TPU v7x, 32 devices: a whole 2x2x4 slice. The times are simulated.
32 devices in a mesh: data: 32 (over z, y, x, core).
Axes of the slice: x: 2, y: 2, z: 4, core: 2. Of those that a mesh axis runs over, the one named last changes fastest.
Arguments:
- grad_attn: bfloat16 [32, 16, 262144], P('data')
- grad_mlp: bfloat16 [32, 8, 1048576], P('data')
- grad_wide: bfloat16 [32, 4, 2048], P('data')
- grad_vec: bfloat16 [32, 38, 512], P('data')
- weight_attn: float32 [16, 262144], P(None, 'data')
- weight_mlp: float32 [8, 1048576], P(None, 'data')
- weight_wide: float32 [4, 2048], P(None, 'data')
- weight_vec: float32 [38, 512], P(None, 'data')
- mom1_attn: float32 [16, 262144], P(None, 'data')
- mom1_mlp: float32 [8, 1048576], P(None, 'data')
- mom1_wide: float32 [4, 2048], P(None, 'data')
- mom1_vec: float32 [38, 512], P(None, 'data')
- mom2_attn: float32 [16, 262144], P(None, 'data')
- mom2_mlp: float32 [8, 1048576], P(None, 'data')
- mom2_wide: float32 [4, 2048], P(None, 'data')
- mom2_vec: float32 [38, 512], P(None, 'data')
Outputs:
- output 1: bfloat16 [16, 262144], replicated
- output 2: bfloat16 [8, 1048576], replicated
- output 3: bfloat16 [4, 2048], replicated
- output 4: bfloat16 [38, 512], replicated
- output 5: float32 [16, 262144], P(None, 'data')
- output 6: float32 [8, 1048576], P(None, 'data')
- output 7: float32 [4, 2048], P(None, 'data')
- output 8: float32 [38, 512], P(None, 'data')
- output 9: float32 [16, 262144], P(None, 'data')
- output 10: float32 [8, 1048576], P(None, 'data')
- output 11: float32 [4, 2048], P(None, 'data')
- output 12: float32 [38, 512], P(None, 'data')
- output 13: float32 [16, 262144], P(None, 'data')
- output 14: float32 [8, 1048576], P(None, 'data')
- output 15: float32 [4, 2048], P(None, 'data')
- output 16: float32 [38, 512], P(None, 'data')
All inputs are finite; a program needn't handle non-finite values.
Results may differ from a plain program's by a relative error of at most 0.001.
Values are sent between devices in bfloat16 or wider.
A program may use at most 1 GiB of HBM per device.

v0:
```python
import jax
import jax.numpy as jnp
from jax import lax
from jax.sharding import PartitionSpec as P

STEP_NUMBER = 10
LEARN_RATE = 0.04
BETA_FIRST = 0.9
BETA_SECOND = 0.999
EPSILON = 1e-6
WEIGHT_DECAY = 0.01
MAX_NORM = 1.0


def adam_direction(mean_grad, weight, first_moment, second_moment, clip_coef):
    clipped = clip_coef * mean_grad
    new_first = BETA_FIRST * first_moment + (1.0 - BETA_FIRST) * clipped
    new_second = BETA_SECOND * second_moment + (1.0 - BETA_SECOND) * (clipped * clipped)
    update = (new_first / (1.0 - BETA_FIRST ** STEP_NUMBER)) / (jnp.sqrt(new_second / (1.0 - BETA_SECOND ** STEP_NUMBER)) + EPSILON) + WEIGHT_DECAY * weight
    return update, new_first, new_second


def solution(mesh):
    group_size = mesh.shape["data"]
    grad_spec = P("data", None, None)
    shard_spec = P(None, "data")
    full_spec = P(None, None)

    def local_step(*all_banks):
        grad_banks = all_banks[0:4]
        weights = all_banks[4:8]
        firsts = all_banks[8:12]
        seconds = all_banks[12:16]
        mean_grads = []
        for grad_bank in grad_banks:
            row_count = grad_bank.shape[1]
            shard_width = grad_bank.shape[2] // group_size
            by_owner = grad_bank.reshape(row_count, group_size, shard_width)
            received = lax.all_to_all(by_owner, "data", 1, 1, tiled=True)
            mean_grads.append(jnp.sum(received, axis=1, dtype=jnp.float32) / group_size)
        local_square = sum(jnp.sum(mean_grad * mean_grad) for mean_grad in mean_grads)
        clip_coef = jnp.minimum(1.0, MAX_NORM / jnp.sqrt(lax.psum(local_square, "data")))
        results = [adam_direction(mean_grads[bank_index], weights[bank_index], firsts[bank_index], seconds[bank_index], clip_coef) for bank_index in range(4)]
        part_sums = jnp.concatenate([jnp.sum(weight * weight, axis=1) for weight in weights] + [jnp.sum(result[0] * result[0], axis=1) for result in results])
        norm_sums = lax.psum(part_sums, "data")
        tensor_count = norm_sums.shape[0] // 2
        trust_ratios = jnp.sqrt(norm_sums[:tensor_count]) / jnp.sqrt(norm_sums[tensor_count:])
        replicas, new_weights = [], []
        first_row = 0
        for bank_index in range(4):
            row_count = weights[bank_index].shape[0]
            trust_ratio = trust_ratios[first_row:first_row + row_count]
            first_row = first_row + row_count
            new_weight = weights[bank_index] - LEARN_RATE * trust_ratio[:, None] * results[bank_index][0]
            new_weights.append(new_weight)
            replicas.append(lax.all_gather(new_weight.astype(jnp.bfloat16), "data", axis=1, tiled=True))
        return tuple(replicas + new_weights + [result[1] for result in results] + [result[2] for result in results])

    return jax.shard_map(local_step, mesh=mesh, in_specs=(grad_spec,) * 4 + (shard_spec,) * 12, out_specs=(full_spec,) * 4 + (shard_spec,) * 12, check_vma=False)
```

profile of v0, /device:TPU:0, one launch (start us, length us, event | category | flops | bytes accessed | tf_op | source)
XLA Modules:
  0.0 928.4 jit_solution(17351107649580000696)
XLA Ops:
  7.2 0.8 reshape.54
  8.0 0.7 reshape.58
  8.7 7.4 all-to-all-start.2
  16.1 0.9 copy.41
  17.0 0.8 reshape.60
  17.8 5.3 all-to-all-done.2
  23.2 2.6 all-to-all-start.3
  25.8 11.4 %copy.44 = bf16[2,8,32,8192]{3,2,1,0:T(8,128)(2,1)} copy(bf16[2,8,32,8192]{3,1,2,0:T(8,128)(2,1)} %bitcast.22) | data formatting | bytes 16777216
  37.1 11.4 %copy.39 = bf16[16,32,8192]{2,0,1:T(8,128)(2,1)} copy(bf16[16,32,8192]{2,1,0:T(8,128)(2,1)} %bitcast.20) | data formatting | bytes 16777216 | tf_op jit(solution)/shard_map/reshape | solution.py:38
  48.5 0.0 all-to-all-done.3
  48.5 192.4 %all_to_all.20 = bf16[16,32,8192]{2,0,1:T(8,128)(2,1)} all-to-all(bf16[16,32,8192]{2,0,1:T(8,128)(2,1)} %copy.39), channel_id=1, replica_groups=mesh['data'=32] {'data'}, dimensions={1} | all-to-all | bytes 16777216 | tf_op jit(solution)/shard_map/all_to_all | solution.py:39
  240.9 5.0 all-to-all-start.1
  245.9 0.0 copy-start.10
  246.0 0.0 copy-start.11
  246.0 0.0 copy-start.12
  246.0 0.0 copy-start.1
  246.0 0.2 all-gather.4.cloned.1.call-start
  246.2 0.1 reshape.59
  246.4 0.6 multiply_reduce_fusion.10
  247.0 0.2 reshape.61
  247.2 0.6 multiply_reduce_fusion.7
  247.8 4.9 convert_reduce_fusion.1
  252.6 0.7 multiply_reduce_fusion.4
  253.4 341.6 %all-to-all-done.1 = bf16[8,32,32768]{2,0,1:T(8,128)(2,1)} async-done(((bf16[8,32,32768]{2,0,1:T(8,128)(2,1)}), bf16[8,32,32768]{2,0,1:T(8,128)(2,1)}, u32[]{:S(2)}, u32[]{:S(2)}) %all-to-all-start.1) | async-done | bytes 16777248 | tf_op jit(solution)/shard_map/all_to_all | solution.py:39
  595.0 6.7 convert_reduce_fusion
  601.7 0.9 multiply_reduce_fusion.1
  605.2 54.4 %psum.14 = f32[]{:T(128)} all-reduce(f32[]{:T(128)S(6)} %add.75), channel_id=1, replica_groups=mesh['data'=32] {'data'}, use_global_device_ids=true, to_apply=%region_12.0 | all-reduce | flops 1 | bytes 8 | tf_op jit(solution)/shard_map/psum | solution.py:42
  660.3 0.0 copy-done.10
  660.3 0.0 copy-done.11
  660.3 0.0 copy-done.12
  660.4 0.7 multiply_reduce_fusion.9
  661.1 0.0 copy-done.1
  661.1 3.9 multiply_reduce_fusion
  665.0 0.0 copy-done.2
  665.0 1.8 multiply_reduce_fusion.3
  666.7 0.0 copy-done.5
  666.7 0.0 copy-done.8
  666.8 0.0 copy-start.3
  666.8 0.0 copy-start.4
  666.8 0.0 copy-start.6
  666.8 0.0 copy-start.7
  666.8 0.1 concatenate.3
  666.9 42.1 %psum.15 = f32[132]{0:T(256)S(1)} all-reduce(f32[132]{0:T(256)S(1)} %concatenate.3), channel_id=1, replica_groups=mesh['data'=32] {'data'}, use_global_device_ids=true, to_apply=%region_17.0 | all-reduce | flops 132 | bytes 1056 | tf_op jit(solution)/shard_map/psum | solution.py:45
  709.1 0.1 rsqrt_multiply_fusion
  709.1 1.2 fusion.2
  710.3 0.0 all-gather.4.cloned.1.call-update
  710.3 0.0 all-gather.6.cloned.1.call-start
  710.4 0.1 slice_multiply_fusion.2
  710.5 3.3 fusion.1
  713.7 0.0 all-gather.6.cloned.1.call-update
  713.8 0.1 slice_multiply_fusion
  713.8 0.6 fusion
  714.4 40.6 %all_gather.15 = bf16[38,512]{0,1:T(8,128)(2,1)S(1)} all-gather(bf16[38,16]{0,1:T(8,128)(2,1)S(1)} %get-tuple-element.86), channel_id=1, replica_groups=mesh['data'=32] {'data'}, dimensions={1}, use_global_device_ids=true | all-gather | bytes 40128 | tf_op jit(solution)/shard_map/all_gather | solution.py:56
  755.0 0.7 copy.43
  755.8 0.1 slice_multiply_fusion.1
  755.8 0.7 convert_bitcast_fusion
  756.5 36.9 %all-gather = bf16[32,64,4]{1,2,0:T(4,128)(2,1)S(1)} all-gather(bf16[1,64,4]{1,2,0:T(4,128)(2,1)S(1)} %get-tuple-element.88), channel_id=1, replica_groups=mesh['data'=32] {'data'}, dimensions={0}, use_global_device_ids=true | all-gather | bytes 16896 | tf_op jit(solution)/shard_map/all_gather | solution.py:56
  793.4 0.7 reshape.57
  794.1 110.0 %all-gather.6.cloned.1.call-done = bf16[8,1048576]{1,0:T(8,128)(2,1)} async-done(((bf16[8,32768]{1,0:T(8,128)(2,1)}), bf16[8,1048576]{1,0:T(8,128)(2,1)}) %all-gather.6.cloned.1.call-update) | async-done | bytes 16777232 | tf_op jit(solution)/shard_map/all_gather | solution.py:56
  904.0 7.4 copy.49
  911.5 3.9 copy-done
  915.3 6.2 copy.50
  921.5 0.0 copy-done.3
  921.5 0.0 copy-done.6
  (15 shorter events, 0.2 us)
Async XLA Ops:
  8.7 14.5 %all-to-all-start.2 = ((bf16[32,2,128]{2,1,0:T(2,128)(2,1)}), bf16[32,2,128]{2,1,0:T(2,128)(2,1)S(1)}, u32[]{:S(2)}, u32[]{:S(2)}) async-start(bf16[32,2,128]{2,1,0:T(2,128)(2,1)} %reshape.58), calls=%async_computation.2 | async-start | bytes 32768 | tf_op jit(solution)/shard_map/all_to_all | solution.py:39
  23.2 25.3 %all-to-all-start.3 = ((bf16[32,2,304]{2,1,0:T(2,128)(2,1)}), bf16[32,2,304]{2,1,0:T(2,128)(2,1)S(1)}, u32[]{:S(2)}, u32[]{:S(2)}) async-start(bf16[32,2,304]{2,1,0:T(2,128)(2,1)} %reshape.60), calls=%async_computation.3 | async-start | bytes 98304 | tf_op jit(solution)/shard_map/all_to_all | solution.py:39
  240.9 354.1 %all-to-all-start.1 = ((bf16[8,32,32768]{2,0,1:T(8,128)(2,1)}), bf16[8,32,32768]{2,0,1:T(8,128)(2,1)}, u32[]{:S(2)}, u32[]{:S(2)}) async-start(bf16[8,32,32768]{2,0,1:T(8,128)(2,1)} %bitcast.21), calls=%async_computation.1 | async-start | bytes 33554432 | tf_op jit(solution)/shard_map/all_to_all | solution.py:39
  245.9 414.4 %copy-start.10 = (f32[4,64]{1,0:T(4,128)S(1)}, f32[4,64]{1,0:T(4,128)}, u32[]{:S(2)}) copy-start(f32[4,64]{1,0:T(4,128)} %param.22) | copy-start | bytes 3076
  246.0 414.4 %copy-start.11 = (f32[4,64]{1,0:T(4,128)S(1)}, f32[4,64]{1,0:T(4,128)}, u32[]{:S(2)}) copy-start(f32[4,64]{1,0:T(4,128)} %param.26) | copy-start | bytes 3076
  246.0 414.4 %copy-start.12 = (f32[4,64]{1,0:T(4,128)S(1)}, f32[4,64]{1,0:T(4,128)}, u32[]{:S(2)}) copy-start(f32[4,64]{1,0:T(4,128)} %param.30) | copy-start | bytes 3076
  246.0 415.1 %copy-start.1 = (f32[8,32768]{1,0:T(8,128)S(1)}, f32[8,32768]{1,0:T(8,128)}, u32[]{:S(2)}) copy-start(f32[8,32768]{1,0:T(8,128)} %param.21) | copy-start | bytes 3145732
  246.0 548.1 %all-gather.4.cloned.1.call-start = ((), (), s32[]{:S(2)}) async-start(), calls=%async_computation.4 | async-start | bytes 8650752 | tf_op jit(solution)/shard_map/all_gather | solution.py:56
  247.8 417.2 %copy-start.2 = (f32[16,8192]{1,0:T(8,128)S(1)}, f32[16,8192]{1,0:T(8,128)}, u32[]{:S(2)}) copy-start(f32[16,8192]{1,0:T(8,128)} %param.20) | copy-start | bytes 1572868
  247.8 419.0 %copy-start.5 = (f32[38,16]{0,1:T(8,128)S(1)}, f32[38,16]{0,1:T(8,128)}, u32[]{:S(2)}) copy-start(f32[38,16]{0,1:T(8,128)} %param.23) | copy-start | bytes 7300
  247.8 419.0 %copy-start.8 = (f32[38,16]{0,1:T(8,128)S(1)}, f32[38,16]{0,1:T(8,128)}, u32[]{:S(2)}) copy-start(f32[38,16]{0,1:T(8,128)} %param.27) | copy-start | bytes 7300
  247.8 419.0 %copy-start.9 = (f32[38,16]{0,1:T(8,128)S(1)}, f32[38,16]{0,1:T(8,128)}, u32[]{:S(2)}) copy-start(f32[38,16]{0,1:T(8,128)} %param.31) | copy-start | bytes 7300
  666.8 254.8 %copy-start.3 = (f32[16,8192]{1,0:T(8,128)}, f32[16,8192]{1,0:T(8,128)S(1)}, u32[]{:S(2)}) copy-start(f32[16,8192]{1,0:T(8,128)S(1)} %get-tuple-element.129) | copy-start | bytes 1572868
  666.8 254.7 %copy-start.4 = (f32[16,8192]{1,0:T(8,128)}, f32[16,8192]{1,0:T(8,128)S(1)}, u32[]{:S(2)}) copy-start(f32[16,8192]{1,0:T(8,128)S(1)} %get-tuple-element.133) | copy-start | bytes 1572868
  666.8 254.7 %copy-start.6 = (f32[38,16]{0,1:T(8,128)}, f32[38,16]{0,1:T(8,128)S(1)}, u32[]{:S(2)}) copy-start(f32[38,16]{0,1:T(8,128)S(1)} %get-tuple-element.132) | copy-start | bytes 7300
  666.8 254.7 %copy-start.7 = (f32[38,16]{0,1:T(8,128)}, f32[38,16]{0,1:T(8,128)S(1)}, u32[]{:S(2)}) copy-start(f32[38,16]{0,1:T(8,128)S(1)} %get-tuple-element.136) | copy-start | bytes 7300
  710.3 193.7 %all-gather.6.cloned.1.call-start = ((), (), s32[]{:S(2)}) async-start(), calls=%async_computation.5 | async-start | bytes 17301504 | tf_op jit(solution)/shard_map/all_gather | solution.py:56
  904.0 11.3 %copy-start = (bf16[8,1048576]{1,0:T(8,128)(2,1)S(1)}, bf16[8,1048576]{1,0:T(8,128)(2,1)}, u32[]{:S(2)}) copy-start(bf16[8,1048576]{1,0:T(8,128)(2,1)} %all-gather.6.cloned.1.call-done) | copy-start | bytes 50331652
Sparse Core Ops, SparseCore 0:
  710.5 76.6 all-gather.3
  790.6 113.4 all-gather.5
where the time goes:
time: 929 us; the launch traced here: 928 us
  waiting for transfers between devices  457 us (49%)
  blocking collectives  366 us (39%)
  local copies, waits for them, and re-layouts  45.3 us (5%)
  other arithmetic  26.9 us (3%)
  between operations  17.5 us (2%)
  starting transfers between devices  15.2 us (2%)
    all_to_all x3, waiting for transfers between devices, local_step(): received = lax.all_to_all(by_owner, 'data', 1, 1, tiled=True)  347 us
    all_to_all x1, blocking collectives, local_step(): received = lax.all_to_all(by_owner, 'data', 1, 1, tiled=True)  192 us
    all_gather x2, waiting for transfers between devices, local_step(): lax.all_gather(new_weight.astype(jnp.bfloat16), 'data', axis=1, tiled=True)  110 us
    all_gather x2, blocking collectives, local_step(): lax.all_gather(new_weight.astype(jnp.bfloat16), 'data', axis=1, tiled=True)  77.4 us
    psum x1, blocking collectives, local_step(): lax.psum(local_square, 'data')  54.4 us
    psum x1, blocking collectives, local_step(): norm_sums = lax.psum(part_sums, 'data')  42.1 us
    unnamed x36, local copies, waits for them, and re-layouts  33.1 us
  transfers between devices with their start and end apart: 5, of which 3 were waited for; matrix products, arithmetic and copies ran while one was open for 4% of the time, Pallas kernels for 0%

commit v1 on v0

v1 whole, which is shorter than its diff:
```python
import jax
import jax.numpy as jnp
from jax import lax
from jax.sharding import PartitionSpec as P
from jax.experimental import pallas as pl
from jax.experimental.pallas import tpu as pltpu

STEP_NUMBER = 10
LEARN_RATE = 0.04
BETA_FIRST = 0.9
BETA_SECOND = 0.999
EPSILON = 1e-6
WEIGHT_DECAY = 0.01
MAX_NORM = 1.0

CHUNKS = 16
SCRATCHES = 18
DEVICES, HALF, OTHERS = 32, 16, 31
LANES = 128
TILE = (8, 128)
CORE, X, Y, Z0, Z1 = 1, 2, 4, 8, 16
STREAMS = (
    ("mlp", 12288, 20480, (Y, X, Z0, Z1)),
    ("mlp", 0, 12288, (X, Y, Z0, Z1)),
    ("attn", 0, 8192, (Z0, X, Y, Z1)),
)
ROWS = {"attn": 16, "mlp": 8}
SHARD = {"attn": 8192, "mlp": 32768}
MESH = pl.DeviceIdType.MESH
HIGHEST = lax.Precision.HIGHEST


def loop(first, stop, body):
    lax.fori_loop(first, stop, body, 0)


def direction(grad, weight, first, second, clip):
    clipped = clip * grad
    new_first = BETA_FIRST * first + (1.0 - BETA_FIRST) * clipped
    new_second = BETA_SECOND * second + (1.0 - BETA_SECOND) * (clipped * clipped)
    update = (new_first / (1.0 - BETA_FIRST ** STEP_NUMBER)) / (jnp.sqrt(new_second / (1.0 - BETA_SECOND ** STEP_NUMBER)) + EPSILON) + WEIGHT_DECAY * weight
    return update, new_first, new_second


def fold_lanes(value):
    total = value[:, 0:LANES]
    for column in range(LANES, value.shape[1], LANES):
        total = total + value[:, column:column + LANES]
    return total


class Stream:
    def __init__(self, bank, first_column, columns, order):
        self.bank, self.first_column, self.columns, self.order = bank, first_column, columns, order
        self.reduce_order = (order[0], CORE) + order[1:]
        self.rows = ROWS[bank]
        self.width = columns // CHUNKS

    def scratch(self):
        rows, width = self.rows, self.width
        return [
            pltpu.VMEM((2, 16, rows, width), jnp.bfloat16),
            pltpu.VMEM((CHUNKS, 16, rows, width), jnp.bfloat16),
            pltpu.VMEM((2, 16, rows, width), jnp.float32),
            pltpu.VMEM((CHUNKS, 8, rows, width), jnp.float32),
            pltpu.VMEM((CHUNKS, 4, rows, width), jnp.float32),
            pltpu.VMEM((CHUNKS, 2, rows, width), jnp.float32),
            pltpu.VMEM((CHUNKS, 1, rows, width), jnp.float32),
            pltpu.VMEM((3, CHUNKS, rows, width), jnp.float32),
            pltpu.VMEM((CHUNKS, 1, rows, width), jnp.bfloat16),
            pltpu.SemaphoreType.DMA((2,)),
            pltpu.SemaphoreType.DMA((2,)),
            pltpu.SemaphoreType.DMA((5, CHUNKS)),
            pltpu.SemaphoreType.DMA((5,)),
            pltpu.SemaphoreType.DMA((4, CHUNKS)),
            pltpu.SemaphoreType.DMA,
            pltpu.SemaphoreType.DMA,
            pltpu.SemaphoreType.DMA,
            pltpu.SemaphoreType.DMA,
        ]

    def bind(self, refs):
        (self.own, self.land, self.acc, self.part8, self.part4, self.part2, self.part1, self.state, self.narrow,
         self.own_sem, self.core_send, self.recv, self.send, self.gather_recv, self.gather_sent, self.core_sent, self.core_got, self.narrow_sem) = refs


def solution(mesh):
    grad_spec = P("data", None, None)
    shard_spec = P(None, "data")
    full_spec = P(None, None)

    def kernel(*refs):
        grads = {"attn": refs[0], "mlp": refs[1]}
        grad_small = refs[2]
        states = {"attn": refs[3:6], "mlp": refs[6:9]}
        state_small = refs[9]
        replicas = {"attn": refs[10], "mlp": refs[11]}
        replica_small = refs[12]
        news = {"attn": refs[13:16], "mlp": refs[16:19]}
        new_small = refs[19]
        rest = refs[20:]
        streams = []
        for index, spec in enumerate(STREAMS):
            stream = Stream(*spec)
            stream.bind(rest[SCRATCHES * index:SCRATCHES * (index + 1)])
            streams.append(stream)
        (small_land, small_state, small_wide, norm_out, norm_land, tile_out, tile_land, square, row_attn, row_mlp,
         small_send, small_recv, norm_send, norm_recv, tile_send, tile_recv, rep_send, rep_recv, load_sem, store_sem, copy_sem) = rest[SCRATCHES * len(streams):]

        me = lax.axis_index("data")
        bit = {w: (me // w) % 2 for w in (CORE, X, Y, Z0, Z1)}
        peer = {w: me + w - 2 * w * bit[w] for w in bit}

        def owner_at(dims, rel):
            owner = bit[CORE] if CORE not in dims else 0
            for weight in reversed(dims):
                owner = owner + weight * ((bit[weight] + rel) % 2)
                rel = rel // 2
            return owner

        def columns_of(s, owner, k):
            return pl.ds(pl.multiple_of(owner * SHARD[s.bank] + s.first_column + k * s.width, LANES), s.width)

        def remote(src, dst, send_sem, recv_sem, device):
            return pltpu.make_async_remote_copy(src_ref=src, dst_ref=dst, send_sem=send_sem, recv_sem=recv_sem, device_id=(device,), device_id_type=MESH)

        def local(src, dst, sem):
            return pltpu.make_async_copy(src, dst, sem)

        def start_raw(s, k):
            slot = k % 2
            grad = grads[s.bank]

            def body(rel, carry):
                remote(grad.at[0, :, columns_of(s, owner_at(s.reduce_order, HALF + rel), k)], s.land.at[k, rel], s.send.at[0], s.recv.at[0, k], peer[s.order[0]]).start()
                local(grad.at[0, :, columns_of(s, owner_at(s.reduce_order, rel), k)], s.own.at[slot, rel], s.own_sem.at[slot]).start()
                return carry

            loop(0, 16, body)

        def add_raw(s, k):
            slot = k % 2
            local(s.own.at[slot], s.own.at[slot], s.own_sem.at[slot]).wait()
            remote(s.land.at[k], s.land.at[k], s.send.at[0], s.recv.at[0, k], peer[s.order[0]]).wait_recv()

            @pl.when(k >= 2)
            def _():
                remote(s.acc.at[slot, pl.ds(8, 8)], s.part8.at[k], s.core_send.at[slot], s.recv.at[1, k], peer[CORE]).wait_send()

            def body(rel, carry):
                s.acc[slot, rel] = s.own[slot, rel].astype(jnp.float32) + s.land[k, rel].astype(jnp.float32)
                return carry

            loop(8, 16, body)
            remote(s.acc.at[slot, pl.ds(8, 8)], s.part8.at[k], s.core_send.at[slot], s.recv.at[1, k], peer[CORE]).start()
            loop(0, 8, body)

        def add_core(s, k):
            slot = k % 2
            remote(s.acc.at[slot, pl.ds(8, 8)], s.part8.at[k], s.core_send.at[slot], s.recv.at[1, k], peer[CORE]).wait_recv()

            def body(rel, carry):
                s.part8[k, rel] = s.part8[k, rel] + s.acc[slot, rel]
                return carry

            loop(4, 8, body)
            remote(s.part8.at[k, pl.ds(4, 4)], s.part4.at[k], s.send.at[2], s.recv.at[2, k], peer[s.order[1]]).start()
            loop(0, 4, body)

        def add_step(s, k, stage):
            held, got = (s.part8, s.part4) if stage == 2 else (s.part4, s.part2)
            half = 4 if stage == 2 else 2
            nxt = s.part2 if stage == 2 else s.part1
            remote(held.at[k, pl.ds(half, half)], got.at[k], s.send.at[stage], s.recv.at[stage, k], peer[s.order[stage - 1]]).wait_recv()

            def body(rel, carry):
                got[k, rel] = got[k, rel] + held[k, rel]
                return carry

            quarter = half // 2
            loop(quarter, half, body)
            remote(got.at[k, pl.ds(quarter, quarter)], nxt.at[k], s.send.at[stage + 1], s.recv.at[stage + 1, k], peer[s.order[stage]]).start()
            loop(0, quarter, body)

        def add_last(s, k):
            remote(s.part2.at[k, pl.ds(1, 1)], s.part1.at[k], s.send.at[4], s.recv.at[4, k], peer[s.order[3]]).wait_recv()
            grad = (s.part1[k, 0] + s.part2[k, 0]) * (1.0 / 32.0)
            s.part1[k, 0] = grad
            part = fold_lanes(grad * grad)
            for row in range(0, s.rows, 8):
                square[...] += part[row:row + 8]

        def to_all(block_for, land, send_sem, recv_sem):
            def body(d, carry):
                other = (me + d) % DEVICES
                remote(block_for(other), land.at[me], send_sem, recv_sem, other).start()
                return carry

            loop(1, DEVICES, body)

        def from_all(land, send_sem, recv_sem):
            blocks = land.at[pl.ds(0, OTHERS)]
            return remote(blocks, blocks, send_sem, recv_sem, me)

        for s in streams:
            start_raw(s, 0)
        small_land[me] = grad_small[me]
        to_all(lambda other: grad_small.at[other], small_land, small_send, small_recv)
        square[...] = jnp.zeros_like(square)

        def start_state(k, carry):
            for s in streams:
                for which in range(3):
                    local(states[s.bank][which].at[:, pl.ds(pl.multiple_of(s.first_column + k * s.width, LANES), s.width)], s.state.at[which, k], load_sem).start()
            return carry

        loop(0, CHUNKS, start_state)

        def reduce_step(t, carry):
            @pl.when(jnp.logical_and(t >= 3, t < CHUNKS + 3))
            def _():
                for s in streams:
                    add_last(s, t - 3)

            @pl.when(jnp.logical_and(t >= 2, t < CHUNKS + 2))
            def _():
                for s in streams:
                    add_step(s, t - 2, 3)

            @pl.when(jnp.logical_and(t >= 1, t < CHUNKS + 1))
            def _():
                for s in streams:
                    add_step(s, t - 1, 2)

            @pl.when(t + 1 < CHUNKS)
            def _():
                for s in streams:
                    start_raw(s, t + 1)

            @pl.when(t < CHUNKS)
            def _():
                for s in streams:
                    add_raw(s, t)
                for s in streams:
                    add_core(s, t)

            return carry

        loop(0, CHUNKS + 3, reduce_step)

        from_all(small_land, small_send, small_recv).wait_recv()
        small_grad = jnp.zeros(TILE, jnp.float32)
        for d in range(DEVICES):
            small_grad = small_grad + small_land[d].astype(jnp.float32)
        small_grad = small_grad * (1.0 / 32.0)
        norm_out[...] = jnp.sum(square[...] + small_grad * small_grad, axis=0, keepdims=True)
        norm_land[me] = norm_out[...]

        to_all(lambda other: norm_out, norm_land, norm_send, norm_recv)

        for s in streams:
            local(s.state, s.state, load_sem).wait()
        row_attn[...] = jnp.zeros_like(row_attn)
        row_mlp[...] = jnp.zeros_like(row_mlp)
        rows_of = {"attn": row_attn, "mlp": row_mlp}
        for s in streams:
            def weight_rows(k, carry, s=s):
                weight = s.state[0, k]
                rows_of[s.bank][1] += fold_lanes(weight * weight)
                return carry
            loop(0, CHUNKS, weight_rows)

        from_all(norm_land, norm_send, norm_recv).wait_recv()
        total = jnp.zeros((1, LANES), jnp.float32)
        for d in range(DEVICES):
            total = total + norm_land[d]
        clip = jnp.minimum(1.0, MAX_NORM / jnp.sqrt(jnp.sum(total, axis=1, keepdims=True)))

        for s in streams:
            def move(k, carry, s=s):
                update, new_first, new_second = direction(s.part1[k, 0], s.state[0, k], s.state[1, k], s.state[2, k], clip)
                s.part1[k, 0] = update
                s.state[1, k] = new_first
                s.state[2, k] = new_second
                rows_of[s.bank][0] += fold_lanes(update * update)
                return carry
            loop(0, CHUNKS, move)
        small_weight = state_small[0]
        small_update, small_first, small_second = direction(small_grad, small_weight, state_small[1], state_small[2], clip)
        small_state[0] = small_update
        new_small[1] = small_first
        new_small[2] = small_second

        lane = lax.broadcasted_iota(jnp.int32, TILE, 1)
        source = lax.broadcasted_iota(jnp.int32, (LANES, LANES), 0)
        target = lax.broadcasted_iota(jnp.int32, (LANES, LANES), 1)
        gather_update = jnp.where(target == source // 16 + 8, 1.0, 0.0)
        gather_weight = jnp.where(target == source // 16 + 24, 1.0, 0.0)
        tile = jnp.dot(small_update * small_update, gather_update, precision=HIGHEST, preferred_element_type=jnp.float32)
        tile = tile + jnp.dot(small_weight * small_weight, gather_weight, precision=HIGHEST, preferred_element_type=jnp.float32)
        for which, base in ((0, 0), (1, 16)):
            attn_sum = jnp.sum(row_attn[which], axis=1, keepdims=True)
            mlp_sum = jnp.sum(row_mlp[which], axis=1, keepdims=True)
            tile = tile + jnp.where(lane == base, attn_sum[0:8], 0.0) + jnp.where(lane == base + 1, attn_sum[8:16], 0.0) + jnp.where(lane == base + 2, mlp_sum, 0.0)
        tile_out[...] = tile
        tile_land[me] = tile

        to_all(lambda other: tile_out, tile_land, tile_send, tile_recv)

        def start_moments(k, carry):
            for s in streams:
                for which in (1, 2):
                    local(s.state.at[which, k], news[s.bank][which].at[:, pl.ds(pl.multiple_of(s.first_column + k * s.width, LANES), s.width)], store_sem).start()
            return carry

        loop(0, CHUNKS, start_moments)
        from_all(tile_land, tile_send, tile_recv).wait_recv()
        sums = tile_land[0]
        for d in range(1, DEVICES):
            sums = sums + tile_land[d]

        def lane_column(index):
            return jnp.sum(jnp.where(lane == index, sums, 0.0), axis=1, keepdims=True)

        def scale(weight_square, update_square):
            return LEARN_RATE * (jnp.sqrt(weight_square) / jnp.sqrt(update_square))

        scale_attn = jnp.concatenate([scale(lane_column(16), lane_column(0)), scale(lane_column(17), lane_column(1))], axis=0)
        scales = {"attn": scale_attn, "mlp": scale(lane_column(18), lane_column(2))}

        row = lax.broadcasted_iota(jnp.int32, TILE, 0)

        def spread(base):
            single = jnp.where(source == target // 16 + base, 1.0, 0.0)
            wide = jnp.where(jnp.logical_and(source // 4 == target // 64 + base // 4, source < base + 8), 1.0, 0.0)
            per_sixteen = jnp.dot(sums, single, precision=HIGHEST, preferred_element_type=jnp.float32)
            per_sixty_four = jnp.dot(sums, wide, precision=HIGHEST, preferred_element_type=jnp.float32)
            return jnp.where(row < 2, per_sixty_four, per_sixteen)

        filled = row * LANES + lane < 864
        small_scale = scale(jnp.where(filled, spread(24), 1.0), jnp.where(filled, spread(8), 1.0))
        small_new = small_weight - small_scale * small_state[0]
        new_small[0] = small_new
        small_wide[...] = small_new.astype(jnp.bfloat16)

        def gather_send(s, k, j):
            out = replicas[s.bank]
            device = peer[s.order[3 - j]]
            mine = out.at[:, columns_of(s, me, k)]
            remote(s.narrow.at[k, 0], mine, s.gather_sent, s.gather_recv.at[j, k], device).start()

            def body(rel, carry):
                block = out.at[:, columns_of(s, owner_at(s.order, rel), k)]
                remote(block, block, s.gather_sent, s.gather_recv.at[j, k], device).start()
                return carry

            if j > 0:
                loop(1, 2 ** j, body)

        def gather_wait(s, k, j):
            out = replicas[s.bank].at[:, pl.ds(0, s.width * 2 ** j)]
            remote(out, out, s.gather_sent, s.gather_recv.at[j, k], me).wait_recv()

        def core_send(s, k, j):
            out = replicas[s.bank]

            def body(rel, carry):
                block = out.at[:, columns_of(s, owner_at(s.order, rel), k)]
                remote(block, block, s.core_sent, s.core_got, peer[CORE]).start()
                return carry

            loop(2 ** j, 2 ** (j + 1), body)

        def renew(s, k):
            new_weight = s.state[0, k] - scales[s.bank] * s.part1[k, 0]
            s.state[0, k] = new_weight
            s.narrow[k, 0] = new_weight.astype(jnp.bfloat16)

        def first_sends(s, k):
            out = replicas[s.bank]
            mine = out.at[:, columns_of(s, me, k)]
            gather_send(s, k, 0)
            remote(s.narrow.at[k, 0], mine, s.core_sent, s.core_got, peer[CORE]).start()
            local(s.narrow.at[k, 0], mine, s.narrow_sem).start()
            local(s.state.at[0, k], news[s.bank][0].at[:, pl.ds(pl.multiple_of(s.first_column + k * s.width, LANES), s.width)], store_sem).start()

        def gather_step(t, carry):
            @pl.when(t < CHUNKS)
            def _():
                for s in streams:
                    renew(s, t)
                for s in streams:
                    first_sends(s, t)

            for j in (1, 2, 3):
                @pl.when(jnp.logical_and(t >= j, t < CHUNKS + j))
                def _(j=j):
                    for s in streams:
                        gather_wait(s, t - j, j - 1)
                        gather_send(s, t - j, j)
                        core_send(s, t - j, j - 1)

            @pl.when(t >= 4)
            def _():
                for s in streams:
                    gather_wait(s, t - 4, 3)
                    core_send(s, t - 4, 3)

            return carry

        gather_step(0, 0)
        to_all(lambda other: small_wide, replica_small, rep_send, rep_recv)
        local(small_wide, replica_small.at[me], copy_sem).start()
        loop(1, CHUNKS + 4, gather_step)

        for s in streams:
            out = replicas[s.bank]
            half = out.at[:, pl.ds(0, 16 * s.columns)]
            remote(half, half, s.core_sent, s.core_got, me).wait()
            sent = out.at[:, pl.ds(0, 15 * s.columns)]
            remote(sent, sent, s.gather_sent, s.core_got, me).wait_send()
            local(s.narrow, s.narrow, s.narrow_sem).wait()
            remote(s.land, s.land, s.send.at[0], s.recv.at[0, 0], me).wait_send()
            for last in (CHUNKS - 2, CHUNKS - 1):
                slot = last % 2
                remote(s.acc.at[slot, pl.ds(8, 8)], s.part8.at[last], s.core_send.at[slot], s.recv.at[1, last], me).wait_send()
            for stage, part in ((2, s.part4), (3, s.part2), (4, s.part1)):
                remote(part, part, s.send.at[stage], s.recv.at[0, 0], me).wait_send()
            local(s.state, s.state, store_sem).wait()
        from_all(small_land, small_send, small_recv).wait_send()
        from_all(norm_land, norm_send, norm_recv).wait_send()
        from_all(tile_land, tile_send, tile_recv).wait_send()
        from_all(replica_small, rep_send, rep_recv).wait()
        local(small_wide, replica_small.at[me], copy_sem).wait()

    def pack_state(wide, vec):
        flat = jnp.concatenate([wide.reshape(-1), vec.reshape(-1), jnp.zeros((160,), jnp.float32)])
        return flat.reshape(TILE)

    def local_step(*banks):
        grad_attn, grad_mlp, grad_wide, grad_vec = banks[0:4]
        states = [banks[4:8], banks[8:12], banks[12:16]]
        wide = grad_wide.reshape(4, 32, 64).transpose(1, 0, 2).reshape(32, 256)
        vec = grad_vec.reshape(38, 32, 16).transpose(1, 0, 2).reshape(32, 608)
        grad_small = jnp.concatenate([wide, vec, jnp.zeros((32, 160), jnp.bfloat16)], axis=1).reshape(32, 8, LANES)
        state_small = jnp.stack([pack_state(state[2], state[3]) for state in states])
        anywhere = pl.BlockSpec(memory_space=pl.ANY)
        vmem = pl.BlockSpec(memory_space=pltpu.VMEM)
        shape = jax.ShapeDtypeStruct
        scratch = []
        for spec in STREAMS:
            scratch += Stream(*spec).scratch()
        scratch += [
            pltpu.VMEM((32, 8, LANES), jnp.bfloat16),
            pltpu.VMEM((1, 8, LANES), jnp.float32),
            pltpu.VMEM(TILE, jnp.bfloat16),
            pltpu.VMEM((1, LANES), jnp.float32),
            pltpu.VMEM((32, 1, LANES), jnp.float32),
            pltpu.VMEM(TILE, jnp.float32),
            pltpu.VMEM((32, 8, LANES), jnp.float32),
            pltpu.VMEM(TILE, jnp.float32),
            pltpu.VMEM((2, 16, LANES), jnp.float32),
            pltpu.VMEM((2, 8, LANES), jnp.float32),
        ] + [pltpu.SemaphoreType.DMA] * 11
        outs = pl.pallas_call(
            kernel,
            name="lamb",
            out_shape=[
                shape((16, 262144), jnp.bfloat16), shape((8, 1048576), jnp.bfloat16), shape((32, 8, LANES), jnp.bfloat16),
                shape((16, 8192), jnp.float32), shape((16, 8192), jnp.float32), shape((16, 8192), jnp.float32),
                shape((8, 32768), jnp.float32), shape((8, 32768), jnp.float32), shape((8, 32768), jnp.float32),
                shape((3, 8, LANES), jnp.float32),
            ],
            in_specs=[anywhere, anywhere, vmem] + [anywhere] * 6 + [vmem],
            out_specs=[anywhere] * 9 + [vmem],
            scratch_shapes=scratch,
            compiler_params=pltpu.CompilerParams(has_side_effects=True, vmem_limit_bytes=62 * 2 ** 20),
        )(grad_attn, grad_mlp, grad_small, states[0][0], states[1][0], states[2][0], states[0][1], states[1][1], states[2][1], state_small)
        replica_small = outs[2].reshape(32, 1024)
        replica_wide = replica_small[:, 0:256].reshape(32, 4, 64).transpose(1, 0, 2).reshape(4, 2048)
        replica_vec = replica_small[:, 256:864].reshape(32, 38, 16).transpose(1, 0, 2).reshape(38, 512)
        new_small = outs[9].reshape(3, 1024)
        results = [outs[0], outs[1], replica_wide, replica_vec]
        for which in range(3):
            results += [outs[3 + which], outs[6 + which], new_small[which, 0:256].reshape(4, 64), new_small[which, 256:864].reshape(38, 16)]
        return tuple(results)

    return jax.shard_map(local_step, mesh=mesh, in_specs=(grad_spec,) * 4 + (shard_spec,) * 12, out_specs=(full_spec,) * 4 + (shard_spec,) * 12, check_vma=False)
```

time: 929 us -> 395 us (0.43)
  waiting for transfers between devices: 457 us -> 0 us
  blocking collectives: 366 us -> 0 us
  Pallas kernels: 0 us -> 353 us
  other arithmetic: 26.9 us -> 0.7 us
  between operations: 17.5 us -> 0.74 us
  starting transfers between devices: 15.2 us -> 0 us
    pallas_call x0 -> x1, Pallas kernels: none -> 353 us  [local_step(): pl.pallas_call(kernel, name='lamb', out_shape=[shape((16, 262144), jnp.bf...]
    all_to_all x3 -> x0, waiting for transfers between devices: 347 us -> none  [local_step(): received = lax.all_to_all(by_owner, 'data', 1, 1, tiled=True)]
    all_to_all x1 -> x0, blocking collectives: 192 us -> none  [local_step(): received = lax.all_to_all(by_owner, 'data', 1, 1, tiled=True)]
    all_gather x2 -> x0, waiting for transfers between devices: 110 us -> none  [local_step(): lax.all_gather(new_weight.astype(jnp.bfloat16), 'data', axis=1, tiled=True)]
    psum x2 -> x0, blocking collectives: 96.6 us -> none  [the longest x1 54.4 us: local_step(): lax.psum(local_square, 'data')]
    all_gather x2 -> x0, blocking collectives: 77.4 us -> none  [local_step(): lax.all_gather(new_weight.astype(jnp.bfloat16), 'data', axis=1, tiled=True)]
    reduce_sum x12 -> x0, other arithmetic: 20.9 us -> none  [the longest x4 11.7 us: local_step(): mean_grads.append(jnp.sum(received, axis=1, dtype=jnp.float32) / group_size)]
    all_to_all x3 -> x0, starting transfers between devices: 15 us -> none  [local_step(): received = lax.all_to_all(by_owner, 'data', 1, 1, tiled=True)]
  transfers between devices with their start and end apart: 5 -> 0, of which waited for: 3 -> 0; matrix products, arithmetic and copies ran while one was open for 4% -> 0% of each run, Pallas kernels for 0% -> 0%
where the time goes in v1:
time: 395 us; the launch traced here: 394 us
  Pallas kernels  353 us (89%)
  local copies, waits for them, and re-layouts  39.5 us (10%)
    pallas_call x1, Pallas kernels, local_step(): pl.pallas_call(kernel, name='lamb', out_shape=[shape((16, 262144), jnp.bf...  353 us
    unnamed x34, local copies, waits for them, and re-layouts  32.3 us

profile of v1, /device:TPU:0, one launch (start us, length us, event | category | flops | bytes accessed | tf_op | source)
XLA Modules:
  0.0 394.2 jit_solution(6072861156755217660)
XLA Ops:
  0.6 0.9 copy.51
  1.6 0.2 copy.52
  1.8 0.1 copy.53
  2.0 0.8 reshape.83
  2.8 0.1 reshape.84
  2.9 0.1 pad.14.clone
  3.0 0.6 copy.65
  3.6 0.8 copy.54
  4.4 0.1 reshape.89
  4.5 0.8 reshape.88
  5.3 0.8 copy.55
  6.1 0.1 reshape.91
  6.1 0.8 reshape.90
  6.9 0.8 copy.56
  7.7 0.1 reshape.93
  7.8 0.8 reshape.92
  8.5 0.1 fusion
  8.6 0.6 pad_maximum_fusion.refs_9_
  9.2 353.2 %lamb.1 = (bf16[16,262144]{1,0:T(8,128)(2,1)}, bf16[8,1048576]{1,0:T(8,128)(2,1)}, bf16[32,8,128]{2,1,0:T(8,128)(2,1)}, f32[16,8192]{1,0:T(8,128)}, f32[16,8192]...) custom-call(bf16[1,16,262144]{2,1,0:T(8,128)(2,1)} %refs_0_.1, ...), custom_call_target="tpu_custom_call" | custom-call | tf_op jit(solution)/shard_map/lamb/pallas_call | solution.py:465
  362.5 0.9 copy.72
  363.3 0.1 reshape.95
  363.4 0.7 reshape.96
  364.1 0.2 copy.64
  364.3 0.3 copy.59
  364.6 0.7 copy.60
  365.3 0.7 copy.75
  366.0 0.7 reshape_squeeze.18
  366.7 0.1 reshape_squeeze.19
  366.8 0.7 copy.61
  367.5 0.7 reshape_squeeze.20
  368.1 0.1 reshape_squeeze.21
  368.2 0.7 copy.62
  368.9 0.7 reshape_squeeze.22
  369.5 0.1 reshape_squeeze.23
  369.6 0.7 copy.63
  370.3 0.0 copy-start
  370.3 7.4 %copy.84 = bf16[16,262144]{1,0:T(8,128)(2,1)} copy(bf16[16,262144]{1,0:T(8,128)(2,1)} %get-tuple-element.93) | data formatting | bytes 16777216
  377.7 3.9 copy-done
  381.6 0.0 copy-start.6
  381.6 0.0 copy-start.3
  381.6 0.0 copy-start.5
  381.6 0.0 copy-start.2
  381.6 0.0 copy-start.4
  381.6 0.0 copy-start.1
  381.6 7.2 %copy.85 = bf16[8,1048576]{1,0:T(8,128)(2,1)} copy(bf16[8,1048576]{1,0:T(8,128)(2,1)S(1)} %copy-done) | data formatting | bytes 33554432
  388.9 0.0 copy-done.6
  388.9 0.8 copy.86
  389.7 0.0 copy-done.3
  389.7 1.0 copy.87
  390.6 0.0 copy-done.5
  390.6 0.8 copy.88
  391.4 0.0 copy-done.2
  391.4 1.0 copy.89
  392.4 0.0 copy-done.4
  392.4 0.8 copy.90
  393.2 0.0 copy-done.1
  393.2 1.0 copy.91
  (9 shorter events, 0.1 us)
Async XLA Ops:
  370.3 11.3 %copy-start = (bf16[8,1048576]{1,0:T(8,128)(2,1)S(1)}, bf16[8,1048576]{1,0:T(8,128)(2,1)}, u32[]{:S(2)}) copy-start(bf16[8,1048576]{1,0:T(8,128)(2,1)} %get-tuple-element.94) | copy-start | bytes 50331652
  381.6 7.2 %copy-start.6 = (f32[16,8192]{1,0:T(8,128)S(1)}, f32[16,8192]{1,0:T(8,128)}, u32[]{:S(2)}) copy-start(f32[16,8192]{1,0:T(8,128)} %get-tuple-element.97) | copy-start | bytes 1572868
  381.6 8.0 %copy-start.3 = (f32[8,32768]{1,0:T(8,128)S(1)}, f32[8,32768]{1,0:T(8,128)}, u32[]{:S(2)}) copy-start(f32[8,32768]{1,0:T(8,128)} %get-tuple-element.98) | copy-start | bytes 3145732
  381.6 9.0 %copy-start.5 = (f32[16,8192]{1,0:T(8,128)S(1)}, f32[16,8192]{1,0:T(8,128)}, u32[]{:S(2)}) copy-start(f32[16,8192]{1,0:T(8,128)} %get-tuple-element.101) | copy-start | bytes 1572868
  381.6 9.8 %copy-start.2 = (f32[8,32768]{1,0:T(8,128)S(1)}, f32[8,32768]{1,0:T(8,128)}, u32[]{:S(2)}) copy-start(f32[8,32768]{1,0:T(8,128)} %get-tuple-element.102) | copy-start | bytes 3145732
  381.6 10.8 %copy-start.4 = (f32[16,8192]{1,0:T(8,128)S(1)}, f32[16,8192]{1,0:T(8,128)}, u32[]{:S(2)}) copy-start(f32[16,8192]{1,0:T(8,128)} %get-tuple-element.105) | copy-start | bytes 1572868
  381.6 11.6 %copy-start.1 = (f32[8,32768]{1,0:T(8,128)S(1)}, f32[8,32768]{1,0:T(8,128)}, u32[]{:S(2)}) copy-start(f32[8,32768]{1,0:T(8,128)} %get-tuple-element.106) | copy-start | bytes 3145732

commit v2 on v1

v2 whole, which is shorter than its diff:
```python
import jax
import jax.numpy as jnp
from jax import lax
from jax.sharding import PartitionSpec as P
from jax.experimental import pallas as pl
from jax.experimental.pallas import tpu as pltpu

STEP_NUMBER = 10
LEARN_RATE = 0.04
BETA_FIRST = 0.9
BETA_SECOND = 0.999
EPSILON = 1e-6
WEIGHT_DECAY = 0.01
MAX_NORM = 1.0

CHUNKS = 16
AHEAD = 2
SLOTS = AHEAD + 1
SCRATCHES = 14
DEVICES, HALF, OTHERS = 32, 16, 31
LANES = 128
VECTORS = 38
TILE = (8, 128)
CORE, X, Y, Z0, Z1 = 1, 2, 4, 8, 16
STREAMS = (
    ("mlp", 12288, 20480, (Y, X, Z0, Z1)),
    ("mlp", 0, 12288, (X, Y, Z0, Z1)),
    ("attn", 0, 8192, (Z0, X, Y, Z1)),
)
NATURAL = (Z1, Z0, Y, X, CORE)
ROWS = {"attn": 16, "mlp": 8}
SHARD = {"attn": 8192, "mlp": 32768}
MESH = pl.DeviceIdType.MESH
HIGHEST = lax.Precision.HIGHEST


def loop(first, stop, body):
    lax.fori_loop(first, stop, body, 0)


def direction(grad, weight, first, second, clip):
    clipped = clip * grad
    new_first = BETA_FIRST * first + (1.0 - BETA_FIRST) * clipped
    new_second = BETA_SECOND * second + (1.0 - BETA_SECOND) * (clipped * clipped)
    update = (new_first / (1.0 - BETA_FIRST ** STEP_NUMBER)) / (jnp.sqrt(new_second / (1.0 - BETA_SECOND ** STEP_NUMBER)) + EPSILON) + WEIGHT_DECAY * weight
    return update, new_first, new_second


def fold_lanes(value):
    total = value[:, 0:LANES]
    for column in range(LANES, value.shape[1], LANES):
        total = total + value[:, column:column + LANES]
    return total


class Stream:
    def __init__(self, bank, first_column, columns, order):
        self.bank, self.first_column, self.columns, self.order = bank, first_column, columns, order
        self.reduce_order = (order[0], CORE) + order[1:]
        self.rows = ROWS[bank]
        self.width = columns // CHUNKS
        self.tiles = self.rows // 8
        self.kept_dims = [weight for weight in NATURAL if weight != order[0]]

    def scratch(self):
        rows, width = self.rows, self.width
        return [
            pltpu.VMEM((SLOTS, self.tiles, 2, 2, 2, 2, 8, width), jnp.bfloat16),
            pltpu.VMEM((2, 16, rows, width), jnp.float32),
            pltpu.VMEM((CHUNKS, 8, rows, width), jnp.float32),
            pltpu.VMEM((CHUNKS, 4, rows, width), jnp.float32),
            pltpu.VMEM((CHUNKS, 2, rows, width), jnp.float32),
            pltpu.VMEM((CHUNKS, 1, rows, width), jnp.float32),
            pltpu.SemaphoreType.DMA((SLOTS,)),
            pltpu.SemaphoreType.DMA((2,)),
            pltpu.SemaphoreType.DMA((5, CHUNKS)),
            pltpu.SemaphoreType.DMA((5,)),
            pltpu.SemaphoreType.DMA((4, CHUNKS)),
            pltpu.SemaphoreType.DMA((4,)),
            pltpu.SemaphoreType.DMA,
            pltpu.SemaphoreType.DMA,
        ]

    def bind(self, refs, replica, state):
        self.replica, self.state = replica, state
        (self.own, self.acc, self.part8, self.part4, self.part2, self.part1,
         self.own_sem, self.core_send, self.recv, self.send, self.gather_recv, self.gather_sent, self.core_sent, self.core_got) = refs


def solution(mesh):
    grad_spec = P("data", None, None)
    shard_spec = P(None, "data")
    full_spec = P(None, None)

    def kernel(*refs):
        grads = {"attn": refs[0], "mlp": refs[1]}
        grad_wide, grad_vec = refs[2:4]
        given_states = {"attn": refs[4:7], "mlp": refs[7:10]}
        given_wide, given_vec = refs[10:13], refs[13:16]
        replicas = {"attn": refs[16], "mlp": refs[17]}
        replica_wide, replica_vec = refs[18:20]
        states = {"attn": refs[20], "mlp": refs[21]}
        state_wide, state_vec = refs[22:24]
        rest = refs[24:]
        streams = []
        for index, spec in enumerate(STREAMS):
            stream = Stream(*spec)
            stream.bind(rest[SCRATCHES * index:SCRATCHES * (index + 1)], replicas[stream.bank], states[stream.bank])
            streams.append(stream)
        (square_pad, vec_rows, vec_land, wide_land, vec_sums, vec_pack, wide_pack, vec_out, wide_out, vec_got, wide_got, vec_grad,
         norm_out, norm_land, tile_out, tile_land, square, row_attn, row_mlp,
         vec_send, vec_recv, wide_send, wide_recv, norm_send, norm_recv, tile_send, tile_recv,
         vec_sent, vec_back, wide_sent, wide_back, load_sem) = rest[SCRATCHES * len(streams):]

        me = lax.axis_index("data")
        bit = {w: (me // w) % 2 for w in (CORE, X, Y, Z0, Z1)}
        peer = {w: me + w - 2 * w * bit[w] for w in bit}

        def blocks(s, whole, columns, fixed):
            picks = [fixed.get(weight, slice(None)) for weight in NATURAL]
            return whole.at[(slice(None), *picks, slice(None), columns)]

        def chunk(s, k):
            start = s.first_column + k * s.width
            return pl.ds(start if isinstance(k, int) else pl.multiple_of(start, LANES), s.width)

        def every(s):
            return pl.ds(s.first_column, s.columns)

        def remote(src, dst, send_sem, recv_sem, device):
            return pltpu.make_async_remote_copy(src_ref=src, dst_ref=dst, send_sem=send_sem, recv_sem=recv_sem, device_id=(device,), device_id_type=MESH)

        def local(src, dst, sem):
            return pltpu.make_async_copy(src, dst, sem)

        def start_raw(s, k):
            slot = k % SLOTS
            first = s.order[0]
            given, kept = [{first: value} for value in (1 - bit[first], bit[first])]
            remote(blocks(s, grads[s.bank], chunk(s, k), given), blocks(s, s.replica, chunk(s, k), given), s.send.at[0], s.recv.at[0, k], peer[first]).start()
            local(blocks(s, grads[s.bank], chunk(s, k), kept), s.own.at[slot], s.own_sem.at[slot]).start()

        def add_raw(s, k):
            slot = k % 2
            mine = k % SLOTS
            local(s.own.at[mine], s.own.at[mine], s.own_sem.at[mine]).wait()
            first = s.order[0]
            landed = blocks(s, s.replica, chunk(s, k), {first: bit[first]})
            remote(landed, landed, s.send.at[0], s.recv.at[0, k], peer[first]).wait_recv()

            @pl.when(k >= 2)
            def _():
                remote(s.acc.at[slot, pl.ds(8, 8)], s.part8.at[k], s.core_send.at[slot], s.recv.at[1, k], peer[CORE]).wait_send()

            def body(rel, carry):
                place = {}
                left = rel
                for weight in reversed(s.reduce_order[1:]):
                    place[weight] = (bit[weight] + left) % 2
                    left = left // 2
                kept = [place[weight] for weight in s.kept_dims]
                place[first] = bit[first]
                owner = [place[weight] for weight in NATURAL]
                for tile in range(s.tiles):
                    got = s.replica[(tile, *owner, slice(None), chunk(s, k))]
                    s.acc[slot, rel, 8 * tile:8 * tile + 8] = s.own[(mine, tile, *kept)].astype(jnp.float32) + got.astype(jnp.float32)
                return carry

            loop(8, 16, body)
            remote(s.acc.at[slot, pl.ds(8, 8)], s.part8.at[k], s.core_send.at[slot], s.recv.at[1, k], peer[CORE]).start()
            loop(0, 8, body)

        def add_core(s, k):
            slot = k % 2
            remote(s.acc.at[slot, pl.ds(8, 8)], s.part8.at[k], s.core_send.at[slot], s.recv.at[1, k], peer[CORE]).wait_recv()

            def body(rel, carry):
                s.part8[k, rel] = s.part8[k, rel] + s.acc[slot, rel]
                return carry

            loop(4, 8, body)
            remote(s.part8.at[k, pl.ds(4, 4)], s.part4.at[k], s.send.at[2], s.recv.at[2, k], peer[s.order[1]]).start()
            loop(0, 4, body)

        def add_step(s, k, stage):
            held, got = (s.part8, s.part4) if stage == 2 else (s.part4, s.part2)
            half = 4 if stage == 2 else 2
            nxt = s.part2 if stage == 2 else s.part1
            remote(held.at[k, pl.ds(half, half)], got.at[k], s.send.at[stage], s.recv.at[stage, k], peer[s.order[stage - 1]]).wait_recv()

            def body(rel, carry):
                got[k, rel] = got[k, rel] + held[k, rel]
                return carry

            quarter = half // 2
            loop(quarter, half, body)
            remote(got.at[k, pl.ds(quarter, quarter)], nxt.at[k], s.send.at[stage + 1], s.recv.at[stage + 1, k], peer[s.order[stage]]).start()
            loop(0, quarter, body)

        def add_last(s, k):
            remote(s.part2.at[k, pl.ds(1, 1)], s.part1.at[k], s.send.at[4], s.recv.at[4, k], peer[s.order[3]]).wait_recv()
            grad = (s.part1[k, 0] + s.part2[k, 0]) * (1.0 / 32.0)
            s.part1[k, 0] = grad
            part = fold_lanes(grad * grad)
            for row in range(0, s.rows, 8):
                square[...] += part[row:row + 8]

        def to_all(block_for, land, send_sem, recv_sem):
            def body(d, carry):
                other = (me + d) % DEVICES
                remote(block_for(other), land.at[me], send_sem, recv_sem, other).start()
                return carry

            loop(1, DEVICES, body)

        def from_all(land, send_sem, recv_sem):
            blocks = land.at[pl.ds(0, OTHERS)]
            return remote(blocks, blocks, send_sem, recv_sem, me)

        for k in range(AHEAD):
            for s in streams:
                start_raw(s, k)
        for bank in states:
            for which in range(3):
                local(given_states[bank][which], states[bank].at[which], load_sem).start()
        for which in range(3):
            local(given_wide[which], state_wide.at[which], load_sem).start()
            local(given_vec[which], state_vec.at[which], load_sem).start()

        def turned(z):
            return pl.ds(z * LANES, LANES)

        square_pad[...] = jnp.zeros_like(square_pad)
        for z in range(4):
            square_pad[0:VECTORS] = grad_vec[0, :, turned(z)].astype(jnp.float32)
            rows = square_pad[...].T.astype(jnp.bfloat16)
            for place in range(8):
                vec_rows[8 * z + place] = rows[16 * place:16 * place + 16]

        def wide_tile(owner):
            return pl.ds(pl.multiple_of(owner // 2 * LANES, LANES), LANES)

        vec_land[me] = vec_rows[me]
        wide_land[me] = grad_wide[0, :, wide_tile(me)]
        to_all(lambda other: vec_rows.at[other], vec_land, vec_send, vec_recv)
        to_all(lambda other: grad_wide.at[0, :, wide_tile(other)], wide_land, wide_send, wide_recv)
        square[...] = jnp.zeros_like(square)

        stages = (add_raw, add_core, lambda s, k: add_step(s, k, 2), lambda s, k: add_step(s, k, 3), add_last)

        def reduce_step(t, carry):
            @pl.when(t + AHEAD < CHUNKS)
            def _():
                for s in streams:
                    start_raw(s, t + AHEAD)

            for lag in reversed(range(len(stages))):
                @pl.when(jnp.logical_and(t >= lag, t < CHUNKS + lag))
                def _(lag=lag):
                    for s in streams:
                        stages[lag](s, t - lag)

            return carry

        loop(0, CHUNKS + len(stages) - 1, reduce_step)

        from_all(vec_land, vec_send, vec_recv).wait_recv()
        from_all(wide_land, wide_send, wide_recv).wait_recv()

        def sum_all(land):
            total = land[0].astype(jnp.float32)
            for d in range(1, DEVICES):
                total = total + land[d].astype(jnp.float32)
            return total

        vec_full = sum_all(vec_land) * (1.0 / 32.0)
        wide_full = sum_all(wide_land) * (1.0 / 32.0)
        wide_full = jnp.where(bit[CORE] == 0, wide_full, pltpu.roll(wide_full, 64, 1))
        lane_wide = lax.broadcasted_iota(jnp.int32, (4, LANES), 1)
        wide_full = jnp.where(lane_wide < 64, wide_full, 0.0)
        vec_grad[...] = vec_full
        wide_pack[...] = wide_full
        norm_out[...] = (jnp.sum(square[...], axis=0, keepdims=True) + jnp.sum(vec_full * vec_full, axis=0, keepdims=True)
                         + jnp.sum(wide_full * wide_full, axis=0, keepdims=True))
        norm_land[me] = norm_out[...]

        to_all(lambda other: norm_out, norm_land, norm_send, norm_recv)

        for state in (states["attn"], states["mlp"], state_wide, state_vec):
            local(state, state, load_sem).wait()
        row_attn[...] = jnp.zeros_like(row_attn)
        row_mlp[...] = jnp.zeros_like(row_mlp)
        rows_of = {"attn": row_attn, "mlp": row_mlp}
        for s in streams:
            def weight_rows(k, carry, s=s):
                weight = s.state[0, :, chunk(s, k)]
                rows_of[s.bank][1] += fold_lanes(weight * weight)
                return carry
            loop(0, CHUNKS, weight_rows)

        from_all(norm_land, norm_send, norm_recv).wait_recv()
        total = jnp.zeros((1, LANES), jnp.float32)
        for d in range(DEVICES):
            total = total + norm_land[d]
        clip = jnp.minimum(1.0, MAX_NORM / jnp.sqrt(jnp.sum(total, axis=1, keepdims=True)))

        for s in streams:
            def move(k, carry, s=s):
                here = chunk(s, k)
                update, new_first, new_second = direction(s.part1[k, 0], *[s.state[which, :, here] for which in range(3)], clip)
                s.part1[k, 0] = update
                s.state[1, :, here] = new_first
                s.state[2, :, here] = new_second
                rows_of[s.bank][0] += fold_lanes(update * update)
                return carry
            loop(0, CHUNKS, move)
        vec_weight, wide_weight = state_vec[0], state_wide[0]
        vec_update, state_vec[1], state_vec[2] = direction(vec_grad[:, 0:VECTORS], vec_weight, state_vec[1], state_vec[2], clip)
        wide_update, state_wide[1], state_wide[2] = direction(wide_pack[:, 0:64], wide_weight, state_wide[1], state_wide[2], clip)
        vec_pack[...] = jnp.zeros_like(vec_pack)
        for which, value in enumerate((vec_update, vec_weight)):
            vec_pack[0:1, 0:VECTORS] = jnp.sum(value * value, axis=0, keepdims=True)
            vec_sums[which] = pltpu.roll(vec_pack[0:8], 64, 1)

        lane = lax.broadcasted_iota(jnp.int32, TILE, 1)
        row = lax.broadcasted_iota(jnp.int32, TILE, 0)
        tile = vec_sums[0] + pltpu.roll(vec_sums[1], 1, 0)
        wide_sums = [jnp.sum(value * value, axis=1, keepdims=True) for value in (wide_update, wide_weight)]
        wide_pack[...] = jnp.where(lane_wide == 3, wide_sums[0], 0.0) + jnp.where(lane_wide == 19, wide_sums[1], 0.0)
        tile_out[...] = tile
        tile_out[0:4] += wide_pack[...]
        tile = tile_out[...]
        for which, base in ((0, 0), (1, 16)):
            attn_sum = jnp.sum(row_attn[which], axis=1, keepdims=True)
            mlp_sum = jnp.sum(row_mlp[which], axis=1, keepdims=True)
            tile = tile + jnp.where(lane == base, attn_sum[0:8], 0.0) + jnp.where(lane == base + 1, attn_sum[8:16], 0.0) + jnp.where(lane == base + 2, mlp_sum, 0.0)
        tile_out[...] = tile
        tile_land[me] = tile

        to_all(lambda other: tile_out, tile_land, tile_send, tile_recv)

        from_all(tile_land, tile_send, tile_recv).wait_recv()
        sums = tile_land[0]
        for d in range(1, DEVICES):
            sums = sums + tile_land[d]

        def lane_column(index):
            return jnp.sum(jnp.where(lane == index, sums, 0.0), axis=1, keepdims=True)

        def scale(weight_square, update_square):
            return LEARN_RATE * (jnp.sqrt(weight_square) / jnp.sqrt(update_square))

        scale_attn = jnp.concatenate([scale(lane_column(16), lane_column(0)), scale(lane_column(17), lane_column(1))], axis=0)
        scales = {"attn": scale_attn, "mlp": scale(lane_column(18), lane_column(2))}

        turned_sums = pltpu.roll(jnp.where(row < 2, sums, 1.0), 64, 1)
        scale_vec = scale(turned_sums[1:2, 0:VECTORS], turned_sums[0:1, 0:VECTORS])
        vec_new = vec_weight - scale_vec * vec_update
        wide_new = wide_weight - scale(lane_column(19)[0:4], lane_column(3)[0:4]) * wide_update
        state_vec[0] = vec_new
        state_wide[0] = wide_new
        vec_pack[:, 0:VECTORS] = vec_new
        vec_out[...] = vec_pack[...].astype(jnp.bfloat16)
        wide_pack[...] = jnp.zeros_like(wide_pack)
        wide_pack[:, 0:64] = wide_new
        wide_out[...] = (wide_pack[...] + pltpu.roll(wide_pack[...], 64, 1)).astype(jnp.bfloat16)
        vec_got[me] = vec_out[...]
        wide_got[me] = wide_out[...]

        def gathered(s, columns, j, newest=None, core=0):
            fixed = {weight: bit[weight] for weight in s.order[:4 - j]}
            if newest is not None:
                weight = s.order[3 - newest]
                fixed[weight] = 1 - bit[weight]
            fixed[CORE] = (bit[CORE] + core) % 2
            return blocks(s, replicas[s.bank], columns, fixed)

        def gather_send(s, k, j):
            held = gathered(s, chunk(s, k), j)
            remote(held, held, s.gather_sent.at[j], s.gather_recv.at[j, k], peer[s.order[3 - j]]).start()

        def gather_wait(s, k, j):
            got = gathered(s, chunk(s, k), j, j)
            remote(got, got, s.gather_sent.at[j], s.gather_recv.at[j, k], me).wait_recv()

        def core_send(s, k, j):
            got = gathered(s, chunk(s, k), j, j)
            remote(got, got, s.core_sent, s.core_got, peer[CORE]).start()

        def renew(s, k):
            here = chunk(s, k)
            new_weight = s.state[0, :, here] - scales[s.bank] * s.part1[k, 0]
            s.state[0, :, here] = new_weight
            for tile in range(s.tiles):
                s.replica[(tile, *[bit[weight] for weight in NATURAL], slice(None), here)] = new_weight[8 * tile:8 * tile + 8].astype(jnp.bfloat16)

        def first_sends(s, k):
            mine = gathered(s, chunk(s, k), 0)
            gather_send(s, k, 0)
            remote(mine, mine, s.core_sent, s.core_got, peer[CORE]).start()

        def gather_step(t, carry):
            @pl.when(t < CHUNKS)
            def _():
                for s in streams:
                    renew(s, t)
                for s in streams:
                    first_sends(s, t)

            for j in (1, 2, 3):
                @pl.when(jnp.logical_and(t >= j, t < CHUNKS + j))
                def _(j=j):
                    for s in streams:
                        gather_wait(s, t - j, j - 1)
                        gather_send(s, t - j, j)
                        core_send(s, t - j, j - 1)

            @pl.when(t >= 4)
            def _():
                for s in streams:
                    gather_wait(s, t - 4, 3)
                    core_send(s, t - 4, 3)

            return carry

        gather_step(0, 0)
        to_all(lambda other: vec_out, vec_got, vec_sent, vec_back)
        to_all(lambda other: wide_out, wide_got, wide_sent, wide_back)
        loop(1, CHUNKS + 4, gather_step)

        from_all(vec_got, vec_sent, vec_back).wait()
        from_all(wide_got, wide_sent, wide_back).wait()
        for z in range(4):
            for place in range(8):
                square_pad[16 * place:16 * place + 16] = vec_got[8 * z + place].astype(jnp.float32)
            replica_vec[:, turned(z)] = square_pad[...].T[0:VECTORS].astype(jnp.bfloat16)
        for pair in range(HALF):
            low, high = wide_got[2 * pair].astype(jnp.float32), wide_got[2 * pair + 1].astype(jnp.float32)
            replica_wide[:, turned(pair)] = jnp.where(lane_wide < 64, low, high).astype(jnp.bfloat16)

        for s in streams:
            half = gathered(s, every(s), 4)
            remote(half, half, s.core_sent, s.core_got, me).wait()
            for j in range(4):
                held = gathered(s, every(s), j)
                remote(held, held, s.gather_sent.at[j], s.core_got, me).wait_send()
            first = s.order[0]
            landed = blocks(s, s.replica, every(s), {first: bit[first]})
            remote(landed, landed, s.send.at[0], s.recv.at[0, 0], me).wait_send()
            for last in (CHUNKS - 2, CHUNKS - 1):
                slot = last % 2
                remote(s.acc.at[slot, pl.ds(8, 8)], s.part8.at[last], s.core_send.at[slot], s.recv.at[1, last], me).wait_send()
            for stage, part in ((2, s.part4), (3, s.part2), (4, s.part1)):
                remote(part, part, s.send.at[stage], s.recv.at[0, 0], me).wait_send()
        from_all(vec_land, vec_send, vec_recv).wait_send()
        from_all(wide_land, wide_send, wide_recv).wait_send()
        from_all(norm_land, norm_send, norm_recv).wait_send()
        from_all(tile_land, tile_send, tile_recv).wait_send()

    def store(*refs):
        results, outs, sem = refs[:8], refs[8:24], refs[24]
        copies = []
        for index in range(4):
            copies.append((results[index], outs[index]))
            for which in range(3):
                copies.append((results[4 + index].at[which], outs[4 + 4 * which + index]))
        copies = [pltpu.make_async_copy(source, target, sem.at[index]) for index, (source, target) in enumerate(copies)]
        for copy in copies:
            copy.start()
        for copy in copies:
            copy.wait()

    def local_step(*banks):
        grad_attn, grad_mlp, grad_wide, grad_vec = banks[0:4]
        given = [[banks[4 + 4 * which + index] for which in range(3)] for index in range(4)]
        given[3] = [state.T for state in given[3]]
        bits = (2,) * 5
        grad_attn = grad_attn.reshape(2, 8, 32, 8192).transpose(0, 2, 1, 3).reshape(2, *bits, 8, 8192)
        grad_mlp = grad_mlp.reshape(8, 32, 32768).transpose(1, 0, 2).reshape(1, *bits, 8, 32768)
        anywhere = pl.BlockSpec(memory_space=pl.ANY)
        vmem = pl.BlockSpec(memory_space=pltpu.VMEM)
        narrow, wide = jnp.bfloat16, jnp.float32
        scratch = []
        for spec in STREAMS:
            scratch += Stream(*spec).scratch()
        small = [
            ((LANES, LANES), wide), ((DEVICES, HALF, LANES), narrow), ((DEVICES, HALF, LANES), narrow), ((DEVICES, 4, LANES), narrow),
            ((2, *TILE), wide), ((HALF, LANES), wide), ((4, LANES), wide), ((HALF, LANES), narrow), ((4, LANES), narrow),
            ((DEVICES, HALF, LANES), narrow), ((DEVICES, 4, LANES), narrow), ((HALF, LANES), wide),
            ((1, LANES), wide), ((DEVICES, 1, LANES), wide), (TILE, wide), ((DEVICES, *TILE), wide), (TILE, wide),
            ((2, HALF, LANES), wide), ((2, *TILE), wide),
        ]
        scratch += [pltpu.VMEM(*spec) for spec in small] + [pltpu.SemaphoreType.DMA] * 13
        replicas = [(grad_attn.shape, narrow), (grad_mlp.shape, narrow), (grad_wide.shape[1:], narrow), (grad_vec.shape[1:], narrow)]
        states = [((3, *state[0].shape), wide) for state in given]
        results = pl.pallas_call(
            kernel,
            name="lamb",
            out_shape=[pltpu.VMEM(*spec) for spec in replicas + states],
            in_specs=[anywhere, anywhere, vmem, vmem] + [anywhere] * 12,
            out_specs=[vmem] * 8,
            scratch_shapes=scratch,
            compiler_params=pltpu.CompilerParams(has_side_effects=True, vmem_limit_bytes=32 * 2 ** 20),
        )(grad_attn, grad_mlp, grad_wide, grad_vec, *[state for bank in given for state in bank])
        shape = jax.ShapeDtypeStruct
        outs = list(pl.pallas_call(
            store,
            name="store",
            out_shape=[shape(*spec) for spec in replicas] + [shape(spec[0][1:], wide) for spec in states] * 3,
            in_specs=[vmem] * 8,
            out_specs=[anywhere] * 16,
            scratch_shapes=[pltpu.SemaphoreType.DMA((16,))],
            compiler_params=pltpu.CompilerParams(vmem_limit_bytes=2 ** 20),
        )(*results))
        outs[0] = outs[0].reshape(2, 32, 8, 8192).transpose(0, 2, 1, 3).reshape(16, -1)
        outs[1] = outs[1].reshape(32, 8, 32768).transpose(1, 0, 2).reshape(8, -1)
        for index in (7, 11, 15):
            outs[index] = outs[index].T
        return tuple(outs)

    return jax.shard_map(local_step, mesh=mesh, in_specs=(grad_spec,) * 4 + (shard_spec,) * 12, out_specs=(full_spec,) * 4 + (shard_spec,) * 12, check_vma=False)
```

time: 395 us -> 326 us (0.83)
  local copies, waits for them, and re-layouts: 39.5 us -> 0 us
  Pallas kernels: 353 us -> 325 us
    unnamed x34 -> x0, local copies, waits for them, and re-layouts: 32.3 us -> none
    pallas_call x1 -> x2, Pallas kernels: 353 us -> 325 us  [the longest x1 315 us: local_step(): pl.pallas_call(kernel, name='lamb', out_shape=[pltpu.VMEM(*spec) for spec...]
    reshape x13 -> x0, local copies, waits for them, and re-layouts: 4.39 us -> none  [the longest x3 2.29 us: pack_state(): wide.reshape(-1)]
where the time goes in v2:
time: 326 us; the launch traced here: 325 us
  Pallas kernels  325 us (100%)
    pallas_call x1, Pallas kernels, local_step(): pl.pallas_call(kernel, name='lamb', out_shape=[pltpu.VMEM(*spec) for spec...  315 us
    pallas_call x1, Pallas kernels, local_step(): pl.pallas_call(store, name='store', out_shape=[shape(*spec) for spec in r...  10 us

profile of v2, /device:TPU:0, one launch (start us, length us, event | category | flops | bytes accessed | tf_op | source)
XLA Modules:
  0.0 325.3 jit_solution(6858406939339911344)
XLA Ops:
  0.7 314.6 %lamb.1 = (bf16[2,2,2,2,2,2,8,8192]{7,6,5,4,3,2,1,0:T(8,128)(2,1)S(1)}, bf16[1,2,2,2,2,2,8,32768]{7,6,5,4,3,2,1,0:T(8,128)(2,1)S(1)}, bf16[4,2048]{1,0:T(4,128)(...) custom-call(bf16[2,2,2,2,2,2,8,8192]{7,6,5,4,3,2,1,0:T(8,128)(2,1)} , ...), custom_call_target="tpu_custom_call" | custom-call | tf_op jit(solution)/shard_map/lamb/pallas_call | solution.py:496
  315.2 10.0 %store.1 = (bf16[2,2,2,2,2,2,8,8192]{7,6,5,4,3,2,1,0:T(8,128)(2,1)}, bf16[1,2,2,2,2,2,8,32768]{7,6,5,4,3,2,1,0:T(8,128)(2,1)}, bf16[4,2048]{1,0:T(4,128)(2,1)}, ...) custom-call(bf16[2,2,2,2,2,2,8,8192]{7,6,5,4,3,2,1,0:T(8,128)(2,1)S(, ...), custom_call_target="tpu_custom_call" | custom-call | tf_op jit(solution)/shard_map/store/pallas_call | solution.py:506

commit v3 on v2

--- a/solution.py
+++ b/solution.py
@@ -13,8 +13,7 @@
 WEIGHT_DECAY = 0.01
 MAX_NORM = 1.0
 
-CHUNKS = 16
-AHEAD = 2
+AHEAD = 1
 SLOTS = AHEAD + 1
 SCRATCHES = 14
 DEVICES, HALF, OTHERS = 32, 16, 31
@@ -22,10 +21,13 @@
 VECTORS = 38
 TILE = (8, 128)
 CORE, X, Y, Z0, Z1 = 1, 2, 4, 8, 16
-STREAMS = (
-    ("mlp", 12288, 20480, (Y, X, Z0, Z1)),
-    ("mlp", 0, 12288, (X, Y, Z0, Z1)),
-    ("attn", 0, 8192, (Z0, X, Y, Z1)),
+ROUTES = (
+    ("mlp", (Y, X, Z0, Z1), 12288),
+    ("mlp", (X, Y, Z0, Z1), 0),
+    ("attn", (Z0, X, Y, Z1), 0),
+)
+GROUPS = (
+    (16, (10, 6, 4)),
 )
 NATURAL = (Z1, Z0, Y, X, CORE)
 ROWS = {"attn": 16, "mlp": 8}
@@ -53,12 +55,15 @@
     return total
 
 
+TOTAL = sum(chunks for chunks, _ in GROUPS)
+
+
 class Stream:
-    def __init__(self, bank, first_column, columns, order):
-        self.bank, self.first_column, self.columns, self.order = bank, first_column, columns, order
+    def __init__(self, bank, order, first_column, width, chunks, begin, gather_begin):
+        self.bank, self.order, self.first_column, self.width, self.chunks = bank, order, first_column, width, chunks
+        self.columns, self.begin, self.gather_begin = width * chunks, begin, gather_begin
         self.reduce_order = (order[0], CORE) + order[1:]
         self.rows = ROWS[bank]
-        self.width = columns // CHUNKS
         self.tiles = self.rows // 8
         self.kept_dims = [weight for weight in NATURAL if weight != order[0]]
 
@@ -67,15 +72,15 @@
         return [
             pltpu.VMEM((SLOTS, self.tiles, 2, 2, 2, 2, 8, width), jnp.bfloat16),
             pltpu.VMEM((2, 16, rows, width), jnp.float32),
-            pltpu.VMEM((CHUNKS, 8, rows, width), jnp.float32),
-            pltpu.VMEM((CHUNKS, 4, rows, width), jnp.float32),
-            pltpu.VMEM((CHUNKS, 2, rows, width), jnp.float32),
-            pltpu.VMEM((CHUNKS, 1, rows, width), jnp.float32),
+            pltpu.VMEM((self.chunks, 8, rows, width), jnp.float32),
+            pltpu.VMEM((self.chunks, 4, rows, width), jnp.float32),
+            pltpu.VMEM((self.chunks, 2, rows, width), jnp.float32),
+            pltpu.VMEM((self.chunks, 1, rows, width), jnp.float32),
             pltpu.SemaphoreType.DMA((SLOTS,)),
             pltpu.SemaphoreType.DMA((2,)),
-            pltpu.SemaphoreType.DMA((5, CHUNKS)),
+            pltpu.SemaphoreType.DMA((5, self.chunks)),
             pltpu.SemaphoreType.DMA((5,)),
-            pltpu.SemaphoreType.DMA((4, CHUNKS)),
+            pltpu.SemaphoreType.DMA((4, self.chunks)),
             pltpu.SemaphoreType.DMA((4,)),
             pltpu.SemaphoreType.DMA,
             pltpu.SemaphoreType.DMA,
@@ -87,6 +92,18 @@
          self.own_sem, self.core_send, self.recv, self.send, self.gather_recv, self.gather_sent, self.core_sent, self.core_got) = refs
 
 
+def make_streams():
+    streams, begin = [], 0
+    firsts = [route[2] for route in ROUTES]
+    for chunks, tiles in GROUPS:
+        for index, (bank, order, _) in enumerate(ROUTES):
+            width = tiles[index] * LANES
+            streams.append(Stream(bank, order, firsts[index], width, chunks, begin, TOTAL - begin - chunks))
+            firsts[index] += width * chunks
+        begin += chunks
+    return streams
+
+
 def solution(mesh):
     grad_spec = P("data", None, None)
     shard_spec = P(None, "data")
@@ -94,7 +111,7 @@
 
     def kernel(*refs):
         grads = {"attn": refs[0], "mlp": refs[1]}
-        grad_wide, grad_vec = refs[2:4]
+        given_wide_grad, given_vec_grad = refs[2:4]
         given_states = {"attn": refs[4:7], "mlp": refs[7:10]}
         given_wide, given_vec = refs[10:13], refs[13:16]
         replicas = {"attn": refs[16], "mlp": refs[17]}
@@ -102,15 +119,13 @@
         states = {"attn": refs[20], "mlp": refs[21]}
         state_wide, state_vec = refs[22:24]
         rest = refs[24:]
-        streams = []
-        for index, spec in enumerate(STREAMS):
-            stream = Stream(*spec)
+        streams = make_streams()
+        for index, stream in enumerate(streams):
             stream.bind(rest[SCRATCHES * index:SCRATCHES * (index + 1)], replicas[stream.bank], states[stream.bank])
-            streams.append(stream)
-        (square_pad, vec_rows, vec_land, wide_land, vec_sums, vec_pack, wide_pack, vec_out, wide_out, vec_got, wide_got, vec_grad,
+        (square_pad, vec_rows, vec_land, wide_land, vec_sums, vec_pack, wide_pack, vec_out, wide_out, vec_got, wide_got, vec_grad, grad_wide, grad_vec,
          norm_out, norm_land, tile_out, tile_land, square, row_attn, row_mlp,
          vec_send, vec_recv, wide_send, wide_recv, norm_send, norm_recv, tile_send, tile_recv,
-         vec_sent, vec_back, wide_sent, wide_back, load_sem) = rest[SCRATCHES * len(streams):]
+         vec_sent, vec_back, wide_sent, wide_back, load_sem, grad_sem) = rest[SCRATCHES * len(streams):]
 
         me = lax.axis_index("data")
         bit = {w: (me // w) % 2 for w in (CORE, X, Y, Z0, Z1)}
@@ -152,23 +167,25 @@
             def _():
                 remote(s.acc.at[slot, pl.ds(8, 8)], s.part8.at[k], s.core_send.at[slot], s.recv.at[1, k], peer[CORE]).wait_send()
 
-            def body(rel, carry):
-                place = {}
-                left = rel
-                for weight in reversed(s.reduce_order[1:]):
-                    place[weight] = (bit[weight] + left) % 2
-                    left = left // 2
+            def add_block(high, low):
+                place = {first: bit[first]}
+                for bits, weights in ((high, (CORE, s.order[1])), (low, s.order[2:])):
+                    for shift, weight in ((2, weights[0]), (1, weights[1])):
+                        place[weight] = (bit[weight] + bits // shift) % 2
                 kept = [place[weight] for weight in s.kept_dims]
-                place[first] = bit[first]
                 owner = [place[weight] for weight in NATURAL]
                 for tile in range(s.tiles):
                     got = s.replica[(tile, *owner, slice(None), chunk(s, k))]
-                    s.acc[slot, rel, 8 * tile:8 * tile + 8] = s.own[(mine, tile, *kept)].astype(jnp.float32) + got.astype(jnp.float32)
+                    s.acc[slot, 4 * high + low, 8 * tile:8 * tile + 8] = s.own[(mine, tile, *kept)].astype(jnp.float32) + got.astype(jnp.float32)
+
+            def body(high, carry):
+                for low in range(4):
+                    add_block(high, low)
                 return carry
 
-            loop(8, 16, body)
+            loop(2, 4, body)
             remote(s.acc.at[slot, pl.ds(8, 8)], s.part8.at[k], s.core_send.at[slot], s.recv.at[1, k], peer[CORE]).start()
-            loop(0, 8, body)
+            loop(0, 2, body)
 
         def add_core(s, k):
             slot = k % 2
@@ -205,6 +222,21 @@
             for row in range(0, s.rows, 8):
                 square[...] += part[row:row + 8]
 
+        def at(chosen, time, begin, act):
+            for first in sorted({getattr(s, begin) for s in chosen}):
+                group = [s for s in chosen if getattr(s, begin) == first]
+                k = time - first
+
+                def run(group=group, k=k):
+                    for s in group:
+                        act(s, k)
+
+                if isinstance(k, int):
+                    if 0 <= k < group[0].chunks:
+                        run()
+                else:
+                    pl.when(jnp.logical_and(k >= 0, k < group[0].chunks))(run)
+
         def to_all(block_for, land, send_sem, recv_sem):
             def body(d, carry):
                 other = (me + d) % DEVICES
@@ -217,9 +249,14 @@
             blocks = land.at[pl.ds(0, OTHERS)]
             return remote(blocks, blocks, send_sem, recv_sem, me)
 
-        for k in range(AHEAD):
-            for s in streams:
-                start_raw(s, k)
+        barrier = pltpu.get_barrier_semaphore()
+        for weight in NATURAL:
+            pl.semaphore_signal(barrier, inc=1, device_id=(peer[weight],), device_id_type=MESH)
+        pl.semaphore_wait(barrier, len(NATURAL))
+        for t in range(AHEAD):
+            at(streams, t, "begin", start_raw)
+        local(given_wide_grad.at[0], grad_wide, grad_sem).start()
+        local(given_vec_grad.at[0], grad_vec, grad_sem).start()
         for bank in states:
             for which in range(3):
                 local(given_states[bank][which], states[bank].at[which], load_sem).start()
@@ -230,9 +267,11 @@
         def turned(z):
             return pl.ds(z * LANES, LANES)
 
+        local(grad_wide, grad_wide, grad_sem).wait()
+        local(grad_vec, grad_vec, grad_sem).wait()
         square_pad[...] = jnp.zeros_like(square_pad)
         for z in range(4):
-            square_pad[0:VECTORS] = grad_vec[0, :, turned(z)].astype(jnp.float32)
+            square_pad[0:VECTORS] = grad_vec[:, turned(z)].astype(jnp.float32)
             rows = square_pad[...].T.astype(jnp.bfloat16)
             for place in range(8):
                 vec_rows[8 * z + place] = rows[16 * place:16 * place + 16]
@@ -241,28 +280,24 @@
             return pl.ds(pl.multiple_of(owner // 2 * LANES, LANES), LANES)
 
         vec_land[me] = vec_rows[me]
-        wide_land[me] = grad_wide[0, :, wide_tile(me)]
-        to_all(lambda other: vec_rows.at[other], vec_land, vec_send, vec_recv)
-        to_all(lambda other: grad_wide.at[0, :, wide_tile(other)], wide_land, wide_send, wide_recv)
+        wide_land[me] = grad_wide[:, wide_tile(me)]
+        def start_small():
+            to_all(lambda other: vec_rows.at[other], vec_land, vec_send, vec_recv)
+            to_all(lambda other: grad_wide.at[:, wide_tile(other)], wide_land, wide_send, wide_recv)
+
         square[...] = jnp.zeros_like(square)
 
         stages = (add_raw, add_core, lambda s, k: add_step(s, k, 2), lambda s, k: add_step(s, k, 3), add_last)
 
         def reduce_step(t, carry):
-            @pl.when(t + AHEAD < CHUNKS)
-            def _():
-                for s in streams:
-                    start_raw(s, t + AHEAD)
-
+            at(streams, t + AHEAD, "begin", start_raw)
             for lag in reversed(range(len(stages))):
-                @pl.when(jnp.logical_and(t >= lag, t < CHUNKS + lag))
-                def _(lag=lag):
-                    for s in streams:
-                        stages[lag](s, t - lag)
-
+                at(streams, t - lag, "begin", stages[lag])
             return carry
 
-        loop(0, CHUNKS + len(stages) - 1, reduce_step)
+        loop(0, TOTAL - 1, reduce_step)
+        start_small()
+        loop(TOTAL - 1, TOTAL + len(stages) - 1, reduce_step)
 
         from_all(vec_land, vec_send, vec_recv).wait_recv()
         from_all(wide_land, wide_send, wide_recv).wait_recv()
@@ -296,7 +331,7 @@
                 weight = s.state[0, :, chunk(s, k)]
                 rows_of[s.bank][1] += fold_lanes(weight * weight)
                 return carry
-            loop(0, CHUNKS, weight_rows)
+            loop(0, s.chunks, weight_rows)
 
         from_all(norm_land, norm_send, norm_recv).wait_recv()
         total = jnp.zeros((1, LANES), jnp.float32)
@@ -313,7 +348,7 @@
                 s.state[2, :, here] = new_second
                 rows_of[s.bank][0] += fold_lanes(update * update)
                 return carry
-            loop(0, CHUNKS, move)
+            loop(0, s.chunks, move)
         vec_weight, wide_weight = state_vec[0], state_wide[0]
         vec_update, state_vec[1], state_vec[2] = direction(vec_grad[:, 0:VECTORS], vec_weight, state_vec[1], state_vec[2], clip)
         wide_update, state_wide[1], state_wide[2] = direction(wide_pack[:, 0:64], wide_weight, state_wide[1], state_wide[2], clip)
@@ -399,34 +434,27 @@
             gather_send(s, k, 0)
             remote(mine, mine, s.core_sent, s.core_got, peer[CORE]).start()
 
+        def gather_last(s, k):
+            gather_wait(s, k, 3)
+            core_send(s, k, 3)
+
+        def gather_next(s, k, j):
+            gather_wait(s, k, j - 1)
+            gather_send(s, k, j)
+            core_send(s, k, j - 1)
+
         def gather_step(t, carry):
-            @pl.when(t < CHUNKS)
-            def _():
-                for s in streams:
-                    renew(s, t)
-                for s in streams:
-                    first_sends(s, t)
-
+            at(streams, t, "gather_begin", renew)
+            at(streams, t, "gather_begin", first_sends)
             for j in (1, 2, 3):
-                @pl.when(jnp.logical_and(t >= j, t < CHUNKS + j))
-                def _(j=j):
-                    for s in streams:
-                        gather_wait(s, t - j, j - 1)
-                        gather_send(s, t - j, j)
-                        core_send(s, t - j, j - 1)
-
-            @pl.when(t >= 4)
-            def _():
-                for s in streams:
-                    gather_wait(s, t - 4, 3)
-                    core_send(s, t - 4, 3)
-
+                at(streams, t - j, "gather_begin", lambda s, k, j=j: gather_next(s, k, j))
+            at(streams, t - 4, "gather_begin", gather_last)
             return carry
 
         gather_step(0, 0)
         to_all(lambda other: vec_out, vec_got, vec_sent, vec_back)
         to_all(lambda other: wide_out, wide_got, wide_sent, wide_back)
-        loop(1, CHUNKS + 4, gather_step)
+        loop(1, TOTAL, gather_step)
 
         from_all(vec_got, vec_sent, vec_back).wait()
         from_all(wide_got, wide_sent, wide_back).wait()
@@ -438,6 +466,8 @@
             low, high = wide_got[2 * pair].astype(jnp.float32), wide_got[2 * pair + 1].astype(jnp.float32)
             replica_wide[:, turned(pair)] = jnp.where(lane_wide < 64, low, high).astype(jnp.bfloat16)
 
+        loop(TOTAL, TOTAL + 4, gather_step)
+
         for s in streams:
             half = gathered(s, every(s), 4)
             remote(half, half, s.core_sent, s.core_got, me).wait()
@@ -447,7 +477,7 @@
             first = s.order[0]
             landed = blocks(s, s.replica, every(s), {first: bit[first]})
             remote(landed, landed, s.send.at[0], s.recv.at[0, 0], me).wait_send()
-            for last in (CHUNKS - 2, CHUNKS - 1):
+            for last in range(s.chunks - 2, s.chunks):
                 slot = last % 2
                 remote(s.acc.at[slot, pl.ds(8, 8)], s.part8.at[last], s.core_send.at[slot], s.recv.at[1, last], me).wait_send()
             for stage, part in ((2, s.part4), (3, s.part2), (4, s.part1)):
@@ -481,26 +511,27 @@
         vmem = pl.BlockSpec(memory_space=pltpu.VMEM)
         narrow, wide = jnp.bfloat16, jnp.float32
         scratch = []
-        for spec in STREAMS:
-            scratch += Stream(*spec).scratch()
+        streams = make_streams()
+        for stream in streams:
+            scratch += stream.scratch()
         small = [
             ((LANES, LANES), wide), ((DEVICES, HALF, LANES), narrow), ((DEVICES, HALF, LANES), narrow), ((DEVICES, 4, LANES), narrow),
             ((2, *TILE), wide), ((HALF, LANES), wide), ((4, LANES), wide), ((HALF, LANES), narrow), ((4, LANES), narrow),
-            ((DEVICES, HALF, LANES), narrow), ((DEVICES, 4, LANES), narrow), ((HALF, LANES), wide),
+            ((DEVICES, HALF, LANES), narrow), ((DEVICES, 4, LANES), narrow), ((HALF, LANES), wide), (grad_wide.shape[1:], narrow), (grad_vec.shape[1:], narrow),
             ((1, LANES), wide), ((DEVICES, 1, LANES), wide), (TILE, wide), ((DEVICES, *TILE), wide), (TILE, wide),
             ((2, HALF, LANES), wide), ((2, *TILE), wide),
         ]
-        scratch += [pltpu.VMEM(*spec) for spec in small] + [pltpu.SemaphoreType.DMA] * 13
+        scratch += [pltpu.VMEM(*spec) for spec in small] + [pltpu.SemaphoreType.DMA] * 14
         replicas = [(grad_attn.shape, narrow), (grad_mlp.shape, narrow), (grad_wide.shape[1:], narrow), (grad_vec.shape[1:], narrow)]
         states = [((3, *state[0].shape), wide) for state in given]
         results = pl.pallas_call(
             kernel,
             name="lamb",
             out_shape=[pltpu.VMEM(*spec) for spec in replicas + states],
-            in_specs=[anywhere, anywhere, vmem, vmem] + [anywhere] * 12,
+            in_specs=[anywhere] * 16,
             out_specs=[vmem] * 8,
             scratch_shapes=scratch,
-            compiler_params=pltpu.CompilerParams(has_side_effects=True, vmem_limit_bytes=32 * 2 ** 20),
+            compiler_params=pltpu.CompilerParams(has_side_effects=True, collective_id=0, vmem_limit_bytes=32 * 2 ** 20),
         )(grad_attn, grad_mlp, grad_wide, grad_vec, *[state for bank in given for state in bank])
         shape = jax.ShapeDtypeStruct
         outs = list(pl.pallas_call(

time: 326 us -> 316 us (0.969)
  Pallas kernels: 325 us -> 315 us
    pallas_call x1, Pallas kernels: 315 us -> 305 us  [local_step(): pl.pallas_call(kernel, name='lamb', out_shape=[pltpu.VMEM(*spec) for spec...]
where the time goes in v3:
time: 316 us; the launch traced here: 315 us
  Pallas kernels  315 us (100%)
    pallas_call x1, Pallas kernels, local_step(): pl.pallas_call(kernel, name='lamb', out_shape=[pltpu.VMEM(*spec) for spec...  305 us
    pallas_call x1, Pallas kernels, local_step(): pl.pallas_call(store, name='store', out_shape=[shape(*spec) for spec in r...  10 us

profile of v3, /device:TPU:0, one launch (start us, length us, event | category | flops | bytes accessed | tf_op | source)
XLA Modules:
  0.0 315.5 jit_solution(312372255768771968)
XLA Ops:
  0.7 304.8 %lamb.1 = (bf16[2,2,2,2,2,2,8,8192]{7,6,5,4,3,2,1,0:T(8,128)(2,1)S(1)}, bf16[1,2,2,2,2,2,8,32768]{7,6,5,4,3,2,1,0:T(8,128)(2,1)S(1)}, bf16[4,2048]{1,0:T(4,128)(...) custom-call(bf16[2,2,2,2,2,2,8,8192]{7,6,5,4,3,2,1,0:T(8,128)(2,1)} , ...), custom_call_target="tpu_custom_call" | custom-call | tf_op jit(solution)/shard_map/lamb/pallas_call | solution.py:527
  305.4 10.0 %store.1 = (bf16[2,2,2,2,2,2,8,8192]{7,6,5,4,3,2,1,0:T(8,128)(2,1)}, bf16[1,2,2,2,2,2,8,32768]{7,6,5,4,3,2,1,0:T(8,128)(2,1)}, bf16[4,2048]{1,0:T(4,128)(2,1)}, ...) custom-call(bf16[2,2,2,2,2,2,8,8192]{7,6,5,4,3,2,1,0:T(8,128)(2,1)S(, ...), custom_call_target="tpu_custom_call" | custom-call | tf_op jit(solution)/shard_map/store/pallas_call | solution.py:537

commit v4 on v3

--- a/solution.py
+++ b/solution.py
@@ -291,13 +291,13 @@
 
         def reduce_step(t, carry):
             at(streams, t + AHEAD, "begin", start_raw)
-            for lag in reversed(range(len(stages))):
+            for lag in range(len(stages)):
                 at(streams, t - lag, "begin", stages[lag])
             return carry
 
-        loop(0, TOTAL - 1, reduce_step)
+        loop(0, TOTAL // 2, reduce_step)
         start_small()
-        loop(TOTAL - 1, TOTAL + len(stages) - 1, reduce_step)
+        loop(TOTAL // 2, TOTAL, reduce_step)
 
         from_all(vec_land, vec_send, vec_recv).wait_recv()
         from_all(wide_land, wide_send, wide_recv).wait_recv()
@@ -315,8 +315,11 @@
         wide_full = jnp.where(lane_wide < 64, wide_full, 0.0)
         vec_grad[...] = vec_full
         wide_pack[...] = wide_full
-        norm_out[...] = (jnp.sum(square[...], axis=0, keepdims=True) + jnp.sum(vec_full * vec_full, axis=0, keepdims=True)
-                         + jnp.sum(wide_full * wide_full, axis=0, keepdims=True))
+        square[0:1] += jnp.sum(vec_full * vec_full, axis=0, keepdims=True) + jnp.sum(wide_full * wide_full, axis=0, keepdims=True)
+
+        loop(TOTAL, TOTAL + len(stages) - 1, reduce_step)
+
+        norm_out[...] = jnp.sum(square[...], axis=0, keepdims=True)
         norm_land[me] = norm_out[...]
 
         to_all(lambda other: norm_out, norm_land, norm_send, norm_recv)
@@ -388,6 +391,57 @@
         scale_attn = jnp.concatenate([scale(lane_column(16), lane_column(0)), scale(lane_column(17), lane_column(1))], axis=0)
         scales = {"attn": scale_attn, "mlp": scale(lane_column(18), lane_column(2))}
 
+        def gathered(s, columns, j, newest=None, core=0):
+            fixed = {weight: bit[weight] for weight in s.order[:4 - j]}
+            if newest is not None:
+                weight = s.order[3 - newest]
+                fixed[weight] = 1 - bit[weight]
+            fixed[CORE] = (bit[CORE] + core) % 2
+            return blocks(s, replicas[s.bank], columns, fixed)
+
+        def gather_send(s, k, j):
+            held = gathered(s, chunk(s, k), j)
+            remote(held, held, s.gather_sent.at[j], s.gather_recv.at[j, k], peer[s.order[3 - j]]).start()
+
+        def gather_wait(s, k, j):
+            got = gathered(s, chunk(s, k), j, j)
+            remote(got, got, s.gather_sent.at[j], s.gather_recv.at[j, k], me).wait_recv()
+
+        def core_send(s, k, j):
+            got = gathered(s, chunk(s, k), j, j)
+            remote(got, got, s.core_sent, s.core_got, peer[CORE]).start()
+
+        def renew(s, k):
+            here = chunk(s, k)
+            new_weight = s.state[0, :, here] - scales[s.bank] * s.part1[k, 0]
+            s.state[0, :, here] = new_weight
+            for tile in range(s.tiles):
+                s.replica[(tile, *[bit[weight] for weight in NATURAL], slice(None), here)] = new_weight[8 * tile:8 * tile + 8].astype(jnp.bfloat16)
+
+        def first_sends(s, k):
+            mine = gathered(s, chunk(s, k), 0)
+            gather_send(s, k, 0)
+            remote(mine, mine, s.core_sent, s.core_got, peer[CORE]).start()
+
+        def gather_last(s, k):
+            gather_wait(s, k, 3)
+            core_send(s, k, 3)
+
+        def gather_next(s, k, j):
+            gather_wait(s, k, j - 1)
+            gather_send(s, k, j)
+            core_send(s, k, j - 1)
+
+        def gather_step(t, carry):
+            at(streams, t, "gather_begin", renew)
+            at(streams, t, "gather_begin", first_sends)
+            for j in (1, 2, 3):
+                at(streams, t - j, "gather_begin", lambda s, k, j=j: gather_next(s, k, j))
+            at(streams, t - 4, "gather_begin", gather_last)
+            return carry
+
+        loop(0, TOTAL // 2, gather_step)
+
         turned_sums = pltpu.roll(jnp.where(row < 2, sums, 1.0), 64, 1)
         scale_vec = scale(turned_sums[1:2, 0:VECTORS], turned_sums[0:1, 0:VECTORS])
         vec_new = vec_weight - scale_vec * vec_update
@@ -401,60 +455,9 @@
         wide_out[...] = (wide_pack[...] + pltpu.roll(wide_pack[...], 64, 1)).astype(jnp.bfloat16)
         vec_got[me] = vec_out[...]
         wide_got[me] = wide_out[...]
-
-        def gathered(s, columns, j, newest=None, core=0):
-            fixed = {weight: bit[weight] for weight in s.order[:4 - j]}
-            if newest is not None:
-                weight = s.order[3 - newest]
-                fixed[weight] = 1 - bit[weight]
-            fixed[CORE] = (bit[CORE] + core) % 2
-            return blocks(s, replicas[s.bank], columns, fixed)
-
-        def gather_send(s, k, j):
-            held = gathered(s, chunk(s, k), j)
-            remote(held, held, s.gather_sent.at[j], s.gather_recv.at[j, k], peer[s.order[3 - j]]).start()
-
-        def gather_wait(s, k, j):
-            got = gathered(s, chunk(s, k), j, j)
-            remote(got, got, s.gather_sent.at[j], s.gather_recv.at[j, k], me).wait_recv()
-
-        def core_send(s, k, j):
-            got = gathered(s, chunk(s, k), j, j)
-            remote(got, got, s.core_sent, s.core_got, peer[CORE]).start()
-
-        def renew(s, k):
-            here = chunk(s, k)
-            new_weight = s.state[0, :, here] - scales[s.bank] * s.part1[k, 0]
-            s.state[0, :, here] = new_weight
-            for tile in range(s.tiles):
-                s.replica[(tile, *[bit[weight] for weight in NATURAL], slice(None), here)] = new_weight[8 * tile:8 * tile + 8].astype(jnp.bfloat16)
-
-        def first_sends(s, k):
-            mine = gathered(s, chunk(s, k), 0)
-            gather_send(s, k, 0)
-            remote(mine, mine, s.core_sent, s.core_got, peer[CORE]).start()
-
-        def gather_last(s, k):
-            gather_wait(s, k, 3)
-            core_send(s, k, 3)
-
-        def gather_next(s, k, j):
-            gather_wait(s, k, j - 1)
-            gather_send(s, k, j)
-            core_send(s, k, j - 1)
-
-        def gather_step(t, carry):
-            at(streams, t, "gather_begin", renew)
-            at(streams, t, "gather_begin", first_sends)
-            for j in (1, 2, 3):
-                at(streams, t - j, "gather_begin", lambda s, k, j=j: gather_next(s, k, j))
-            at(streams, t - 4, "gather_begin", gather_last)
-            return carry
-
-        gather_step(0, 0)
         to_all(lambda other: vec_out, vec_got, vec_sent, vec_back)
         to_all(lambda other: wide_out, wide_got, wide_sent, wide_back)
-        loop(1, TOTAL, gather_step)
+        loop(TOTAL // 2, TOTAL, gather_step)
 
         from_all(vec_got, vec_sent, vec_back).wait()
         from_all(wide_got, wide_sent, wide_back).wait()
@@ -491,7 +494,10 @@
         results, outs, sem = refs[:8], refs[8:24], refs[24]
         copies = []
         for index in range(4):
-            copies.append((results[index], outs[index]))
+            parts = [(z1, z0) for z1 in range(2) for z0 in range(2)] if index < 2 else [None]
+            for part in parts:
+                pick = (slice(None), *part) if part else slice(None)
+                copies.append((results[index].at[pick], outs[index].at[pick]))
             for which in range(3):
                 copies.append((results[4 + index].at[which], outs[4 + 4 * which + index]))
         copies = [pltpu.make_async_copy(source, target, sem.at[index]) for index, (source, target) in enumerate(copies)]
@@ -540,7 +546,7 @@
             out_shape=[shape(*spec) for spec in replicas] + [shape(spec[0][1:], wide) for spec in states] * 3,
             in_specs=[vmem] * 8,
             out_specs=[anywhere] * 16,
-            scratch_shapes=[pltpu.SemaphoreType.DMA((16,))],
+            scratch_shapes=[pltpu.SemaphoreType.DMA((22,))],
             compiler_params=pltpu.CompilerParams(vmem_limit_bytes=2 ** 20),
         )(*results))
         outs[0] = outs[0].reshape(2, 32, 8, 8192).transpose(0, 2, 1, 3).reshape(16, -1)

time: 316 us -> 314 us (level)
  no operation moved by 1% of the time
where the time goes in v4:
time: 314 us
  Pallas kernels  313 us (100%)
    pallas_call x1, Pallas kernels, local_step(): pl.pallas_call(kernel, name='lamb', out_shape=[pltpu.VMEM(*spec) for spec...  303 us
    pallas_call x1, Pallas kernels, local_step(): pl.pallas_call(store, name='store', out_shape=[shape(*spec) for spec in r...  9.98 us

profile of v4, /device:TPU:0, one launch (start us, length us, event | category | flops | bytes accessed | tf_op | source)
XLA Modules:
  0.0 313.7 jit_solution(7864614220288926441)
XLA Ops:
  0.7 303.0 %lamb.1 = (bf16[2,2,2,2,2,2,8,8192]{7,6,5,4,3,2,1,0:T(8,128)(2,1)S(1)}, bf16[1,2,2,2,2,2,8,32768]{7,6,5,4,3,2,1,0:T(8,128)(2,1)S(1)}, bf16[4,2048]{1,0:T(4,128)(...) custom-call(bf16[2,2,2,2,2,2,8,8192]{7,6,5,4,3,2,1,0:T(8,128)(2,1)} , ...), custom_call_target="tpu_custom_call" | custom-call | tf_op jit(solution)/shard_map/lamb/pallas_call | solution.py:533
  303.7 10.0 %store.1 = (bf16[2,2,2,2,2,2,8,8192]{7,6,5,4,3,2,1,0:T(8,128)(2,1)}, bf16[1,2,2,2,2,2,8,32768]{7,6,5,4,3,2,1,0:T(8,128)(2,1)}, bf16[4,2048]{1,0:T(4,128)(2,1)}, ...) custom-call(bf16[2,2,2,2,2,2,8,8192]{7,6,5,4,3,2,1,0:T(8,128)(2,1)S(, ...), custom_call_target="tpu_custom_call" | custom-call | tf_op jit(solution)/shard_map/store/pallas_call | solution.py:543

commit v5 on v4

--- a/solution.py
+++ b/solution.py
@@ -22,13 +22,11 @@
 TILE = (8, 128)
 CORE, X, Y, Z0, Z1 = 1, 2, 4, 8, 16
 ROUTES = (
+    ("attn", (Z0, X, Y, Z1), 0),
+    ("mlp", (X, Y, Z0, Z1), 0),
     ("mlp", (Y, X, Z0, Z1), 12288),
-    ("mlp", (X, Y, Z0, Z1), 0),
-    ("attn", (Z0, X, Y, Z1), 0),
 )
-GROUPS = (
-    (16, (10, 6, 4)),
-)
+GROUPS = ((16,(4,6,10)),)
 NATURAL = (Z1, Z0, Y, X, CORE)
 ROWS = {"attn": 16, "mlp": 8}
 SHARD = {"attn": 8192, "mlp": 32768}

time: 314 us -> 313 us (level)
  no operation moved by 1% of the time
where the time goes in v5:
time: 313 us
  Pallas kernels  312 us (100%)
    pallas_call x1, Pallas kernels, local_step(): pl.pallas_call(kernel, name='lamb', out_shape=[pltpu.VMEM(*spec) for spec...  302 us
    pallas_call x1, Pallas kernels, local_step(): pl.pallas_call(store, name='store', out_shape=[shape(*spec) for spec in r...  9.98 us

profile of v5, /device:TPU:0, one launch (start us, length us, event | category | flops | bytes accessed | tf_op | source)
XLA Modules:
  0.0 312.6 jit_solution(17920284033660225271)
XLA Ops:
  0.7 301.9 %lamb.1 = (bf16[2,2,2,2,2,2,8,8192]{7,6,5,4,3,2,1,0:T(8,128)(2,1)S(1)}, bf16[1,2,2,2,2,2,8,32768]{7,6,5,4,3,2,1,0:T(8,128)(2,1)S(1)}, bf16[4,2048]{1,0:T(4,128)(...) custom-call(bf16[2,2,2,2,2,2,8,8192]{7,6,5,4,3,2,1,0:T(8,128)(2,1)} , ...), custom_call_target="tpu_custom_call" | custom-call | tf_op jit(solution)/shard_map/lamb/pallas_call | solution.py:531
  302.6 10.0 %store.1 = (bf16[2,2,2,2,2,2,8,8192]{7,6,5,4,3,2,1,0:T(8,128)(2,1)}, bf16[1,2,2,2,2,2,8,32768]{7,6,5,4,3,2,1,0:T(8,128)(2,1)}, bf16[4,2048]{1,0:T(4,128)(2,1)}, ...) custom-call(bf16[2,2,2,2,2,2,8,8192]{7,6,5,4,3,2,1,0:T(8,128)(2,1)S(, ...), custom_call_target="tpu_custom_call" | custom-call | tf_op jit(solution)/shard_map/store/pallas_call | solution.py:541
